TPU v7x, 32 devices: a 4x4x1 block of a 4x4x8 slice. The times are simulated.
32 devices in a mesh: rep: 1 (over z), dp: 32 (over x, y, core).
Axes of the slice: x: 4, y: 4, z: 1, core: 2. Of those that a mesh axis runs over, the one named last changes fastest.
The devices are a block of a 4x4x8 slice.
Arguments:
- g_w_gate: bfloat16 [32, 2, 768, 3072], P(('rep', 'dp'))
- g_w_up: bfloat16 [32, 2, 768, 3072], P(('rep', 'dp'))
- g_w_down: bfloat16 [32, 2, 3072, 768], P(('rep', 'dp'))
- w_gate: bfloat16 [2, 768, 3072], replicated
- w_up: bfloat16 [2, 768, 3072], replicated
- w_down: bfloat16 [2, 3072, 768], replicated
- m_w_gate: float32 [2, 768, 3072], P(None, 'dp')
- m_w_up: float32 [2, 768, 3072], P(None, 'dp')
- m_w_down: float32 [2, 3072, 768], P(None, 'dp')
- v_w_gate: float32 [2, 768, 3072], P(None, 'dp')
- v_w_up: float32 [2, 768, 3072], P(None, 'dp')
- v_w_down: float32 [2, 3072, 768], P(None, 'dp')
Outputs:
- output 1: bfloat16 [2, 768, 3072], P('rep')
- output 2: bfloat16 [2, 768, 3072], P('rep')
- output 3: bfloat16 [2, 3072, 768], P('rep')
- output 4: float32 [2, 768, 3072], P('rep', 'dp')
- output 5: float32 [2, 768, 3072], P('rep', 'dp')
- output 6: float32 [2, 3072, 768], P('rep', 'dp')
- output 7: float32 [2, 768, 3072], P('rep', 'dp')
- output 8: float32 [2, 768, 3072], P('rep', 'dp')
- output 9: float32 [2, 3072, 768], P('rep', 'dp')
All inputs are finite; a program needn't handle non-finite values.
Results may differ from a plain program's by a relative error of at most 0.022.
Values are sent between devices in bfloat16 or wider.
A program may use at most 768 MiB of HBM per device.

v0:
```python
import jax
import jax.numpy as jnp
from jax import lax
from jax.sharding import PartitionSpec as P


def adamw(w, m, v, g):
    m = 0.9 * m + 0.1 * g
    v = 0.95 * v + 0.05 * g * g
    step = m * lax.rsqrt(v + 1e-8) + 0.1 * w
    return (w - 0.02 * step).astype(jnp.bfloat16), m, v


def clipped(gradients, sum_of_squares, count):
    factor = jnp.minimum(1.0, 0.5 * lax.rsqrt(sum_of_squares / count + 1e-30))
    return [g * factor for g in gradients]


def solution(mesh):
    def step(*arrays):
        terms, weights, m, v = (arrays[i : i + 3] for i in (0, 3, 6, 9))
        gradients = [lax.psum_scatter(t[0], "dp", scatter_dimension=1, tiled=True).astype(jnp.float32) for t in terms]
        squares = lax.psum(sum(jnp.sum(g * g) for g in gradients), "dp")
        gradients = clipped(gradients, squares, lax.psum(1, "dp") * sum(g.size for g in gradients))
        me = lax.axis_index("dp")
        own = [lax.dynamic_slice_in_dim(w, me * one.shape[1], one.shape[1], 1).astype(jnp.float32) for w, one in zip(weights, m, strict=True)]
        new = [adamw(w, m, v, g) for w, m, v, g in zip(own, m, v, gradients, strict=True)]
        whole = [lax.all_gather(one[0], "dp", axis=1, tiled=True) for one in new]
        return (*whole, *(one[1] for one in new), *(one[2] for one in new))

    all_of, cut = P(None, None, None), P(None, "dp", None)
    return jax.shard_map(
        step,
        mesh=mesh,
        in_specs=(P(("rep", "dp"), None, None, None),) * 3 + (all_of,) * 3 + (cut,) * 6,
        out_specs=(P("rep", None, None),) * 3 + (P("rep", "dp", None),) * 6,
        check_vma=False,
    )
```

profile of v0, /device:TPU:97, one launch (start us, length us, event | category | flops | bytes accessed | tf_op | source)
XLA Modules:
  0.0 544.1 jit_solution(12900120163436808450)
XLA Ops:
  7.2 0.1 reduce-scatter.10.cloned.1.call-start
  7.3 18.3 %copy.21 = bf16[2,768,3072]{2,0,1:T(2,128)(2,1)} copy(bf16[2,768,3072]{2,1,0:T(8,128)(2,1)} %bitcast.15) | data formatting | bytes 18874368
  25.5 10.5 %copy.25 = bf16[96,8,2,3072]{3,1,2,0:T(8,128)(2,1)} copy(bf16[96,8,2,3072]{3,2,1,0:T(2,128)(2,1)} %bitcast.13) | data formatting | bytes 18874368
  36.0 0.1 reduce-scatter.10.cloned.1.call-update
  36.1 0.1 reduce-scatter.12.cloned.1.call-start
  36.2 18.3 %copy.23 = bf16[2,768,3072]{2,0,1:T(2,128)(2,1)} copy(bf16[2,768,3072]{2,1,0:T(8,128)(2,1)} %bitcast.16) | data formatting | bytes 18874368
  54.5 10.5 %copy.26 = bf16[96,8,2,3072]{3,1,2,0:T(8,128)(2,1)} copy(bf16[96,8,2,3072]{3,2,1,0:T(2,128)(2,1)} %bitcast.14) | data formatting | bytes 18874368
  65.0 0.1 reduce-scatter.12.cloned.1.call-update
  65.1 0.1 reduce-scatter.8.cloned.1.call-start
  65.2 0.7 reduce-scatter.8.cloned.1.call-update
  65.9 0.1 all-gather.8.cloned.1.call-start
  66.0 60.2 %reduce-scatter.10.cloned.1.call-done = bf16[24,6144]{1,0:T(8,128)(2,1)} async-done(((bf16[768,6144]{1,0:T(8,128)(2,1)}), bf16[24,6144]{1,0:T(8,128)(2,1)}) %reduce-scatter.10.cloned.1.call-update) | async-done | bytes 294928
  126.2 1.2 reshape.19
  127.4 90.2 %reduce-scatter.12.cloned.1.call-done = bf16[24,6144]{1,0:T(8,128)(2,1)} async-done(((bf16[768,6144]{1,0:T(8,128)(2,1)}), bf16[24,6144]{1,0:T(8,128)(2,1)}) %reduce-scatter.12.cloned.1.call-update) | async-done | bytes 294928
  217.6 1.2 reshape.21
  218.8 0.8 fusion.9
  220.8 87.5 %reduce-scatter.8.cloned.1.call-done = bf16[2,96,768]{2,1,0:T(8,128)(2,1)} async-done(((bf16[2,3072,768]{2,1,0:T(8,128)(2,1)}), bf16[2,96,768]{2,1,0:T(8,128)(2,1)}) %reduce-scatter.8.cloned.1.call-update) | async-done | bytes 294928 | tf_op jit(solution)/shard_map/reduce_scatter | solution.py:22
  308.4 1.7 fusion.11
  310.7 46.5 %psum.7 = f32[]{:T(128)} all-reduce(f32[]{:T(128)S(6)} %add.65), channel_id=1, replica_groups=mesh['rep'=1,'dp'=32] {'dp'}, use_global_device_ids=true, to_apply=%region_6.0 | all-reduce | flops 1 | bytes 8 | tf_op jit(solution)/shard_map/psum | solution.py:23
  357.9 2.3 fusion.17
  360.3 0.1 all-gather.8.cloned.1.call-update
  360.3 0.2 all-gather.4.cloned.1.call-start
  360.6 2.2 fusion.8
  362.8 0.1 all-gather.4.cloned.1.call-update
  362.9 0.1 all-gather.6.cloned.1.call-start
  363.0 2.4 fusion.14
  365.5 43.2 %all-gather.8.cloned.1.call-done = bf16[2,3072,768]{2,1,0:T(8,128)(2,1)} async-done(((bf16[2,96,768]{2,1,0:T(8,128)(2,1)}), bf16[2,3072,768]{2,1,0:T(8,128)(2,1)}) %all-gather.8.cloned.1.call-update) | async-done | bytes 9437200 | tf_op jit(solution)/shard_map/all_gather | solution.py:28
  408.7 51.9 %all-gather.4.cloned.1.call-done = bf16[2,768,3072]{2,1,0:T(8,128)(2,1)} async-done(((bf16[2,24,3072]{2,1,0:T(8,128)(2,1)}), bf16[2,768,3072]{2,1,0:T(8,128)(2,1)}) %all-gather.4.cloned.1.call-update) | async-done | bytes 9437200 | tf_op jit(solution)/shard_map/all_gather | solution.py:28
  460.7 51.9 %all-gather.6.cloned.1.call-done = bf16[2,768,3072]{2,1,0:T(8,128)(2,1)} async-done(((bf16[2,24,3072]{2,1,0:T(8,128)(2,1)}), bf16[2,768,3072]{2,1,0:T(8,128)(2,1)}) %all-gather.6.cloned.1.call-update) | async-done | bytes 9437200 | tf_op jit(solution)/shard_map/all_gather | solution.py:28
  512.6 8.3 %copy.40 = bf16[2,768,3072]{2,1,0:T(8,128)(2,1)} copy(bf16[2,768,3072]{2,1,0:T(8,128)(2,1)} %all-gather.4.cloned.1.call-done) | data formatting | bytes 18874368
  520.9 8.3 %copy.41 = bf16[2,768,3072]{2,1,0:T(8,128)(2,1)} copy(bf16[2,768,3072]{2,1,0:T(8,128)(2,1)} %all-gather.6.cloned.1.call-done) | data formatting | bytes 18874368
  529.2 8.0 %copy.42 = bf16[2,3072,768]{2,1,0:T(8,128)(2,1)} copy(bf16[2,3072,768]{2,1,0:T(8,128)(2,1)} %all-gather.8.cloned.1.call-done) | data formatting | bytes 18874368
  (11 shorter events, 0.1 us)
Async XLA Ops:
  7.2 119.0 %reduce-scatter.10.cloned.1.call-start = ((), (), s32[]{:S(2)}) async-start(), calls=%async_computation.7 | async-start | bytes 9732096
  36.1 181.5 %reduce-scatter.12.cloned.1.call-start = ((), (), s32[]{:S(2)}) async-start(), calls=%async_computation.8 | async-start | bytes 9732096
  65.0 292.9 %copy-start = (f32[2,96,768]{2,1,0:T(8,128)S(1)}, f32[2,96,768]{2,1,0:T(8,128)}, u32[]{:S(2)}) copy-start(f32[2,96,768]{2,1,0:T(8,128)} %param.23) | copy-start | bytes 1769476
  65.0 293.0 %copy-start.1 = (f32[2,96,768]{2,1,0:T(8,128)S(1)}, f32[2,96,768]{2,1,0:T(8,128)}, u32[]{:S(2)}) copy-start(f32[2,96,768]{2,1,0:T(8,128)} %param.20) | copy-start | bytes 1769476
  65.0 295.5 %copy-start.2 = (f32[2,24,3072]{2,1,0:T(8,128)S(1)}, f32[2,24,3072]{2,1,0:T(8,128)}, u32[]{:S(2)}) copy-start(f32[2,24,3072]{2,1,0:T(8,128)} %param.21) | copy-start | bytes 1769476
  65.1 295.5 %copy-start.3 = (f32[2,24,3072]{2,1,0:T(8,128)S(1)}, f32[2,24,3072]{2,1,0:T(8,128)}, u32[]{:S(2)}) copy-start(f32[2,24,3072]{2,1,0:T(8,128)} %param.18) | copy-start | bytes 1769476
  65.1 297.9 %copy-start.4 = (f32[2,24,3072]{2,1,0:T(8,128)S(1)}, f32[2,24,3072]{2,1,0:T(8,128)}, u32[]{:S(2)}) copy-start(f32[2,24,3072]{2,1,0:T(8,128)} %param.22) | copy-start | bytes 1769476
  65.1 243.3 %reduce-scatter.8.cloned.1.call-start = ((), (), s32[]{:S(2)}) async-start(), calls=%async_computation.3 | async-start | bytes 9732096 | tf_op jit(solution)/shard_map/reduce_scatter | solution.py:22
  65.9 342.9 %all-gather.8.cloned.1.call-start = ((), (), s32[]{:S(2)}) async-start(), calls=%async_computation.6 | async-start | bytes 9732096 | tf_op jit(solution)/shard_map/all_gather | solution.py:28
  360.3 100.3 %all-gather.4.cloned.1.call-start = ((), (), s32[]{:S(2)}) async-start(), calls=%async_computation.4 | async-start | bytes 9732096 | tf_op jit(solution)/shard_map/all_gather | solution.py:28
  362.9 149.7 %all-gather.6.cloned.1.call-start = ((), (), s32[]{:S(2)}) async-start(), calls=%async_computation.5 | async-start | bytes 9732096 | tf_op jit(solution)/shard_map/all_gather | solution.py:28
Sparse Core Ops, SparseCore 0:
  36.2 89.9 reduce-scatter.9
  130.3 87.1 reduce-scatter.11
  221.2 87.1 reduce-scatter.7
  360.4 48.2 all-gather.7
  411.3 49.3 all-gather.3
  463.2 49.3 all-gather.5
where the time goes:
time: 545 us; the launch traced here: 544 us
  waiting for transfers between devices  386 us (71%)
  local copies, waits for them, and re-layouts  84.6 us (16%)
  blocking collectives  46.5 us (9%)
  between operations  16.9 us (3%)
  other arithmetic  9.52 us (2%)
    unnamed x8, waiting for transfers between devices  151 us
    all_gather x3, waiting for transfers between devices, step(): whole = [lax.all_gather(one[0], 'dp', axis=1, tiled=True) for one in new]  147 us
    reduce_scatter x1, waiting for transfers between devices, step(): lax.psum_scatter(t[0], 'dp', scatter_dimension=1, tiled=True)  87.5 us
    unnamed x19, local copies, waits for them, and re-layouts  84.6 us
    psum x1, blocking collectives, step(): squares = lax.psum(sum((jnp.sum(g * g) for g in gradients)), 'dp')  46.5 us
  transfers between devices with their start and end apart: 6, of which 6 were waited for; matrix products, arithmetic and copies ran while one was open for 7% of the time, Pallas kernels for 0%

commit v1 on v0

v1 whole, which is shorter than its diff:
```python
import functools
import math

import jax
import jax.numpy as jnp
from jax import lax
from jax.experimental import pallas as pl
from jax.experimental.pallas import tpu as pltpu
from jax.sharding import PartitionSpec as P

LANES = 128
TILE = 8
CORES = 2
AXES = 2
HALVES = 2
QUARTERS = AXES * HALVES
F32, BF16 = jnp.float32, jnp.bfloat16


def tiled(a, *blocks):
    layers, rows, columns = a.shape
    a = a.reshape(layers, rows // TILE, TILE, columns // LANES, LANES).transpose(0, 1, 3, 2, 4)
    return a.reshape(layers, *blocks, rows * columns // (LANES * math.prod(blocks)), LANES)


def untiled(a, shape):
    layers, rows, columns = shape
    a = a.reshape(layers, rows // TILE, columns // LANES, TILE, LANES).transpose(0, 1, 3, 2, 4)
    return a.reshape(shape)


def steps(count, body):
    def run(i, carry):
        body(i)
        return carry

    lax.fori_loop(0, count, run, 0)


def exchange_kernel(n, side, *refs):
    g_refs, w_refs, m_refs, v_refs = (refs[i : i + 3] for i in (0, 3, 6, 9))
    whole, moments = refs[12:14]
    (land1, land2, grads, w_own, m_own, v_own, squares) = refs[14:21]
    (load_sem, swap_send, swap_recv, send1, recv1, send2, recv2, state_sem, sq_send, sq_recv) = refs[21:31]
    (out_send1, out_send2, out_recv, pair_send, pair_recv) = refs[31:]
    kinds = len(g_refs)
    layers = g_refs[0].shape[0]
    rows = g_refs[0].shape[-2] // QUARTERS
    unit = kinds * rows

    me = lax.axis_index("dp")
    core = lax.rem(me, CORES)
    here = (lax.div(lax.div(me, CORES), side), lax.rem(lax.div(me, CORES), side))
    sibling = me + 1 - 2 * core

    def wrap(i):
        return lax.rem(i + 2 * side, side)

    def split(i):
        a, h = i // HALVES, i % HALVES
        return a, h, (1 - a) * here[0] + a * here[1], (1 - a) * here[1] + a * here[0]

    def chip(a, d, e):
        return (1 - a) * d + a * e, (1 - a) * e + a * d

    def device(a, d, e):
        x, y = chip(a, d, e)
        return (x * side + y) * CORES + core

    def remote(src, dst, send, recv, to):
        return pltpu.make_async_remote_copy(
            src_ref=src, dst_ref=dst, send_sem=send, recv_sem=recv, device_id={"dp": to}, device_id_type=pl.DeviceIdType.MESH
        )

    def quarter(i):
        return pl.ds(pl.multiple_of(i * rows, rows), rows)

    def away(s, h):
        return (2, 1 - 2 * h, 2 * h - 1, 0)[s]

    def load(a, h, d, w):
        lines = pl.ds((a * HALVES + h) * rows, rows)
        src = g_refs[w].at[:, d, :, core, lines, :] if a == 0 else g_refs[w].at[:, :, d, core, lines, :]
        return pltpu.make_async_copy(src, whole.at[0, a, h, d, :, :, pl.ds(w * rows, rows), :], load_sem.at[a, h, d, w])

    def swap(a, h, d, w):
        lines = pl.ds((a * HALVES + h) * rows, rows)
        src = g_refs[w].at[:, d, :, 1 - core, lines, :] if a == 0 else g_refs[w].at[:, :, d, 1 - core, lines, :]
        dst = whole.at[1, a, h, d, :, :, pl.ds(w * rows, rows), :]
        return remote(src, dst, swap_send.at[a, h, d, w], swap_recv.at[a, h, d, w], sibling)

    def first(a):
        return here[a]

    def dest(kind, a, h):
        return (wrap(first(a) + 2), wrap(first(a) + 1 - 2 * h), wrap(first(a) + 2 * h - 1), first(a))[kind]

    quarters = [(a, h) for a in range(AXES) for h in range(HALVES)]
    for kind in range(4):
        for a, h in quarters:
            for w in range(kinds):
                load(a, h, dest(kind, a, h), w).start()

    def state_copies():
        mine = (slice(None), here[0], here[1], core)
        for w in range(kinds):
            yield pltpu.make_async_copy(w_refs[w].at[mine], w_own.at[w], state_sem.at[0, w])
            yield pltpu.make_async_copy(m_refs[w], m_own.at[w], state_sem.at[1, w])
            yield pltpu.make_async_copy(v_refs[w], v_own.at[w], state_sem.at[2, w])

    barrier = pltpu.get_barrier_semaphore()

    def greet(i):
        pl.semaphore_signal(barrier, inc=1, device_id={"dp": lax.rem(me + 1 + i, n)}, device_id_type=pl.DeviceIdType.MESH)

    steps(n - 1, greet)
    pl.semaphore_wait(barrier, n - 1)

    for kind in range(4):
        for a, h in quarters:
            for w in range(kinds):
                swap(a, h, dest(kind, a, h), w).start()
    for copy in state_copies():
        copy.start()

    def wait_terms(kind, i):
        a, h, p, _ = split(i)
        d = wrap(p + away(kind, h))

        def one(w):
            pltpu.make_async_copy(whole.at[0, a, h, d, :, :, quarter(w), :], whole.at[0, a, h, d, :, :, quarter(w), :], load_sem.at[a, h, d, w]).wait()
            remote(
                whole.at[1, a, h, d, :, :, quarter(w), :],
                whole.at[1, a, h, d, :, :, quarter(w), :],
                swap_send.at[a, h, d, w],
                swap_recv.at[a, h, d, w],
                sibling,
            ).wait_recv()

        steps(kinds, one)

    def add(dst, *srcs):
        def piece(j):
            at = (j // kinds, quarter(j % kinds))
            total = srcs[0][at].astype(F32)
            for src in srcs[1:]:
                total += src[at].astype(F32)
            dst[at] = total.astype(BF16)

        steps(layers * kinds, piece)

    def toward(kind, p, h):
        return wrap(p + (2 * h - 1, 1 - 2 * h, 2 * h - 1)[kind])

    def pass1(kind, i, s):
        a, h, p, q = split(i)
        d, e = wrap(p + away(kind, h)), wrap(q + away(s, h))
        terms = whole.at[0, a, h, d, :, e]
        return terms, whole.at[1, a, h, d, :, e], remote(
            terms, land1.at[kind, a, h, s], send1.at[kind, a, h, s], recv1.at[kind, a, h, s], device(a, toward(kind, p, h), q)
        )

    for kind in range(3):

        def start1(i):
            a, h, _, _ = split(i)
            if kind < 2:
                wait_terms(kind, i)
            for s in range(4):
                terms, others, copy = pass1(kind, i, s)
                if kind == 2:
                    if s == 0:
                        wait_terms(kind, i)
                    pass1(0, i, s)[2].wait_recv()
                    add(terms, terms, others, land1.at[0, a, h, s])
                else:
                    add(terms, terms, others)
                copy.start()

        steps(QUARTERS, start1)

    def pass2(kind, i):
        a, h, p, q = split(i)
        e = wrap(q + away(kind, h))
        return remote(whole.at[0, a, h, p, :, e], land2.at[kind, a, h], send2.at[kind, a, h], recv2.at[kind, a, h], device(a, p, toward(kind, q, h)))

    for kind in range(3):

        def start2(i):
            a, h, p, q = split(i)
            if kind == 0:
                wait_terms(3, i)
            e = wrap(q + away(kind, h))
            pass1(1, i, kind)[2].wait_recv()
            pass1(2, i, kind)[2].wait_recv()
            terms = whole.at[0, a, h, p, :, e]
            srcs = [terms, whole.at[1, a, h, p, :, e], land1.at[1, a, h, kind], land1.at[2, a, h, kind]]
            if kind == 2:
                pass2(0, i).wait_recv()
                srcs.append(land2.at[0, a, h])
            add(terms, *srcs)
            pass2(kind, i).start()

        steps(QUARTERS, start2)

    def finish(i, total):
        a, h, p, q = split(i)
        pass1(1, i, 3)[2].wait_recv()
        pass1(2, i, 3)[2].wait_recv()
        pass2(1, i).wait_recv()
        pass2(2, i).wait_recv()
        srcs = [whole.at[k, a, h, p, :, q] for k in range(2)] + [land1.at[k, a, h, 3] for k in (1, 2)] + [land2.at[k, a, h] for k in (1, 2)]

        def piece(j, total):
            at = (j // kinds, quarter(j % kinds))
            g = srcs[0][at].astype(F32)
            for src in srcs[1:]:
                g += src[at].astype(F32)
            g = g.astype(BF16)
            grads[a, h, j // kinds, quarter(j % kinds)] = g
            g = g.astype(F32)
            return total + jnp.sum((g * g).reshape(rows // TILE, TILE, LANES), axis=0)

        return lax.fori_loop(0, layers * kinds, piece, total)

    squares[me] = lax.fori_loop(0, QUARTERS, finish, jnp.zeros((TILE, LANES), F32))

    def sent1(j):
        i, s = j // 4, j % 4
        a, h = i // HALVES, i % HALVES
        for kind in range(3):
            remote(land1.at[kind, a, h, s], land1.at[kind, a, h, s], send1.at[kind, a, h, s], recv1.at[kind, a, h, s], sibling).wait_send()

    steps(QUARTERS * 4, sent1)

    def sent2(i):
        for kind in range(3):
            pass2(kind, i).wait_send()

    steps(QUARTERS, sent2)

    def square(i):
        to, by = lax.rem(me + 1 + i, n), lax.rem(me + n - 1 - i, n)
        return (
            remote(squares.at[me], squares.at[me], sq_send.at[i], sq_recv.at[me], to),
            remote(squares.at[me], squares.at[by], sq_send.at[i], sq_recv.at[by], to),
        )

    steps(n - 1, lambda i: square(i)[0].start())
    for copy in state_copies():
        copy.wait()
    steps(n - 1, lambda i: square(i)[1].wait_recv())
    total = lax.fori_loop(0, n, lambda i, t: t + squares[i], jnp.zeros((TILE, LANES), F32))
    total = jnp.sum(jnp.sum(total, axis=0, keepdims=True), axis=1, keepdims=True)
    count = n * layers * kinds * QUARTERS * rows * LANES
    factor = jnp.minimum(1.0, 0.5 * lax.rsqrt(total / count + 1e-30))

    def out2(i, d, e, k, slot, r):
        a, h, p, q = split(i)
        return remote(whole.at[0, a, h, d, :, e], whole.at[0, a, h, d, :, e], out_send2.at[a, h, r, slot], out_recv.at[a, h, d, e], device(a, wrap(p + k), q))

    def out1(i, e, k, slot):
        a, h, p, q = split(i)
        return remote(whole.at[0, a, h, p, :, e], whole.at[0, a, h, p, :, e], out_send1.at[a, h, slot], out_recv.at[a, h, p, e], device(a, p, wrap(q + k)))

    def pair(i, d, e):
        a, h, _, _ = split(i)
        return remote(whole.at[0, a, h, d, :, e], whole.at[1, a, h, d, :, e], pair_send.at[a, h, d, e], pair_recv.at[a, h, d, e], sibling)

    def arrived(i, d, e):
        a, h, p, q = split(i)
        remote(whole.at[0, a, h, d, :, e], whole.at[0, a, h, d, :, e], out_send1.at[a, h, 0], out_recv.at[a, h, d, e], sibling).wait_recv()

    def update(i):
        a, h, p, q = split(i)

        def piece(j):
            layer, w = j // kinds, j % kinds
            at = (w, layer, pl.ds(pl.multiple_of(i * rows, rows), rows))
            g = grads[a, h, layer, quarter(w)].astype(F32) * factor
            w_old = w_own[at].astype(F32)
            m = 0.9 * m_own[at] + 0.1 * g
            v = 0.95 * v_own[at] + 0.05 * g * g
            step = m * lax.rsqrt(v + 1e-8) + 0.1 * w_old
            moments[(0, *at)] = m
            moments[(1, *at)] = v
            whole[0, a, h, p, layer, q, quarter(w)] = (w_old - 0.02 * step).astype(BF16)

        steps(layers * kinds, piece)
        out1(i, q, 2 * h - 1, 0).start()
        out2(i, p, q, 2 * h - 1, 0, 0).start()

    steps(QUARTERS, update)

    def own(i):
        _, h, p, q = split(i)
        out1(i, q, 1 - 2 * h, 1).start()
        out2(i, p, q, 1 - 2 * h, 1, 0).start()
        pair(i, p, q).start()

    steps(QUARTERS, own)

    def place(r, h):
        return (0, 1 - 2 * h, 2 * h - 1, 2)[r]

    def column(r):
        def run(i):
            _, h, p, q = split(i)
            e = wrap(q + place(r, h))
            arrived(i, p, e)
            if r == 1:
                out1(i, e, 2 * h - 1, 2).start()
            out2(i, p, e, 2 * h - 1, 0, r).start()
            out2(i, p, e, 1 - 2 * h, 1, r).start()
            pair(i, p, e).start()

        steps(QUARTERS, run)

    def beside(r):
        def run(i):
            _, h, p, q = split(i)
            e = wrap(q + place(r, h))
            d = wrap(p + 1 - 2 * h)
            arrived(i, d, e)
            out2(i, d, e, 2 * h - 1, 2, r).start()
            pair(i, d, e).start()
            d = wrap(p + 2 * h - 1)
            arrived(i, d, e)
            pair(i, d, e).start()

        steps(QUARTERS, run)

    def across(r):
        def run(i):
            _, h, p, q = split(i)
            d, e = wrap(p + 2), wrap(q + place(r, h))
            arrived(i, d, e)
            pair(i, d, e).start()

        steps(QUARTERS, run)

    column(1)
    column(2)
    beside(0)
    column(3)
    beside(1)
    beside(2)
    across(0)
    beside(3)
    across(1)
    across(2)
    across(3)

    def done(i):
        a, h, p, q = split(i)
        for slot in range(3):
            out1(i, q, 1, slot).wait_send()
            for r in range(4):
                out2(i, p, q, 1, slot, r).wait_send()

        def places(j):
            d, e = j // side, j % side
            pair(i, d, e).wait()

        steps(side * side, places)
        for d in range(side):
            for w in range(kinds):
                remote(
                    whole.at[1, a, h, d, :, :, quarter(w), :],
                    whole.at[1, a, h, d, :, :, quarter(w), :],
                    swap_send.at[a, h, d, w],
                    swap_recv.at[a, h, d, w],
                    sibling,
                ).wait_send()

    steps(QUARTERS, done)
    steps(n - 1, lambda i: square(i)[0].wait_send())


def write_kernel(side, whole, moments, *refs):
    w_refs, m_refs, v_refs, sem = refs[:3], refs[3:6], refs[6:9], refs[9]
    kinds = len(w_refs)
    rows = w_refs[0].shape[-2] // QUARTERS
    core = lax.rem(lax.axis_index("dp"), CORES)

    def copies(d, start):
        count = 0
        for k in range(CORES):
            c = core if k == 0 else 1 - core
            for a in range(AXES):
                for h in range(HALVES):
                    lines = pl.ds((a * HALVES + h) * rows, rows)
                    for w in range(kinds):
                        dst = w_refs[w].at[:, d, :, c, lines, :] if a == 0 else w_refs[w].at[:, :, d, c, lines, :]
                        copy = pltpu.make_async_copy(whole.at[k, a, h, d, :, :, pl.ds(w * rows, rows), :], dst, sem.at[d, count])
                        count += 1
                        copy.start() if start else copy.wait()

    def states():
        for w in range(kinds):
            yield pltpu.make_async_copy(moments.at[0, w], m_refs[w], sem.at[side, w])
            yield pltpu.make_async_copy(moments.at[1, w], v_refs[w], sem.at[side, kinds + w])

    for copy in states():
        copy.start()
    steps(side, lambda d: copies(d, True))
    for copy in states():
        copy.wait()
    steps(side, lambda d: copies(d, False))


def solution(mesh):
    n = mesh.shape["dp"]
    side = math.isqrt(n // CORES)

    def step(*arrays):
        terms, weights, m, v = (arrays[i : i + 3] for i in (0, 3, 6, 9))
        kinds, layers = len(weights), weights[0].shape[0]
        g = [tiled(t[0], side, side, CORES) for t in terms]
        w = [tiled(a, side, side, CORES) for a in weights]
        states = [tiled(a) for a in (*m, *v)]
        block = g[0].shape[-2]
        rows = block // QUARTERS
        unit = kinds * rows
        hbm, vmem = pl.BlockSpec(memory_space=pltpu.HBM), pl.BlockSpec(memory_space=pltpu.VMEM)
        dma = pltpu.SemaphoreType.DMA
        piece = (AXES, HALVES)
        whole, moments = pl.pallas_call(
            functools.partial(exchange_kernel, n, side),
            out_shape=(
                pltpu.VMEM((CORES, *piece, side, layers, side, unit, LANES), BF16),
                pltpu.VMEM((2, kinds, layers, block, LANES), F32),
            ),
            in_specs=[hbm] * 12,
            out_specs=(vmem, vmem),
            scratch_shapes=[
                pltpu.VMEM((3, *piece, side, layers, unit, LANES), BF16),
                pltpu.VMEM((3, *piece, layers, unit, LANES), BF16),
                pltpu.VMEM((*piece, layers, unit, LANES), BF16),
                pltpu.VMEM((kinds, layers, block, LANES), BF16),
                pltpu.VMEM((kinds, layers, block, LANES), F32),
                pltpu.VMEM((kinds, layers, block, LANES), F32),
                pltpu.VMEM((n, TILE, LANES), F32),
                dma((*piece, side, kinds)),
                dma((*piece, side, kinds)),
                dma((*piece, side, kinds)),
                dma((3, *piece, side)),
                dma((3, *piece, side)),
                dma((3, *piece)),
                dma((3, *piece)),
                dma((3, kinds)),
                dma((n,)),
                dma((n,)),
                dma((*piece, 3)),
                dma((*piece, side, 3)),
                dma((*piece, side, side)),
                dma((*piece, side, side)),
                dma((*piece, side, side)),
            ],
            compiler_params=pltpu.CompilerParams(collective_id=0, has_side_effects=True, vmem_limit_bytes=28 << 20),
            name="exchange",
        )(*g, *w, *states)
        out = pl.pallas_call(
            functools.partial(write_kernel, side),
            out_shape=tuple(jax.ShapeDtypeStruct(a.shape, a.dtype) for a in (*w, *states)),
            in_specs=[vmem] * 2,
            out_specs=(hbm,) * 9,
            scratch_shapes=[dma((side + 1, CORES * QUARTERS * kinds))],
            compiler_params=pltpu.CompilerParams(vmem_limit_bytes=1 << 20),
            name="write",
        )(*(pltpu.with_memory_space_constraint(a, pltpu.VMEM) for a in (whole, moments)))
        return tuple(untiled(o, a.shape) for o, a in zip(out, (*weights, *m, *v), strict=True))

    all_of, cut = P(None, None, None), P(None, "dp", None)
    return jax.shard_map(
        step,
        mesh=mesh,
        in_specs=(P(("rep", "dp"), None, None, None),) * 3 + (all_of,) * 3 + (cut,) * 6,
        out_specs=(P("rep", None, None),) * 3 + (P("rep", "dp", None),) * 6,
        check_vma=False,
    )
```

time: 545 us -> 208 us (0.38)
  waiting for transfers between devices: 386 us -> 0 us
  Pallas kernels: 0 us -> 189 us
  local copies, waits for them, and re-layouts: 84.6 us -> 18.4 us
  blocking collectives: 46.5 us -> 0 us
  between operations: 16.9 us -> 0.66 us
  other arithmetic: 9.52 us -> 0 us
    pallas_call x0 -> x2, Pallas kernels: none -> 189 us  [the longest x1 177 us: step(): pl.pallas_call(functools.partial(exchange_kernel, n, side), out_shape=(pl...]
    unnamed x8 -> x0, waiting for transfers between devices: 151 us -> none
    all_gather x3 -> x0, waiting for transfers between devices: 147 us -> none  [step(): whole = [lax.all_gather(one[0], 'dp', axis=1, tiled=True) for one in new]]
    reduce_scatter x1 -> x0, waiting for transfers between devices: 87.5 us -> none  [step(): lax.psum_scatter(t[0], 'dp', scatter_dimension=1, tiled=True)]
    unnamed x19 -> x4, local copies, waits for them, and re-layouts: 84.6 us -> 18.4 us
    psum x1 -> x0, blocking collectives: 46.5 us -> none  [step(): squares = lax.psum(sum((jnp.sum(g * g) for g in gradients)), 'dp')]
    convert_element_type x3 -> x0, other arithmetic: 7.02 us -> none  [adamw(): return ((w - 0.02 * step).astype(jnp.bfloat16), m, v)]
  transfers between devices with their start and end apart: 6 -> 0, of which waited for: 6 -> 0; matrix products, arithmetic and copies ran while one was open for 7% -> 0% of each run, Pallas kernels for 0% -> 0%
where the time goes in v1:
time: 208 us
  Pallas kernels  189 us (91%)
  local copies, waits for them, and re-layouts  18.4 us (9%)
    pallas_call x1, Pallas kernels, step(): pl.pallas_call(functools.partial(exchange_kernel, n, side), out_shape=(pl...  177 us
    unnamed x4, local copies, waits for them, and re-layouts  18.4 us
    pallas_call x1, Pallas kernels, step(): pl.pallas_call(functools.partial(write_kernel, side), out_shape=tuple((ja...  11.4 us

profile of v1, /device:TPU:97, one launch (start us, length us, event | category | flops | bytes accessed | tf_op | source)
XLA Modules:
  0.0 207.9 jit_solution(13019083009685423194)
XLA Ops:
  0.6 177.4 %exchange.1 = (bf16[2,2,2,4,2,4,432,128]{7,6,5,4,3,2,1,0:T(8,128)(2,1)S(1)}, f32[2,3,2,576,128]{4,3,2,1,0:T(8,128)S(1)}) custom-call(bf16[2,4,4,2,576,128]{5,4,3,2,1,0:T(8,128)(2,1)} %bitcast.105, bf16[2,4,4,2,576,128]{5,4,3,2,1,0:T(8,128)(2,1)} %bitcast.106, bf16[2,4,4,2,576,128]{5,4,3,2,1,0:T(8,128)(2,1)} %bitcast.107, ...), custom_call_target="tpu_custom_call" | custom-call | tf_op jit(solution)/shard_map/exchange/pallas_call | solution.py:428
  178.1 0.0 copy-start
  178.1 9.3 %copy-done = bf16[2,2,2,4,2,4,432,128]{7,6,5,4,3,2,1,0:T(8,128)(2,1)} copy-done((bf16[2,2,2,4,2,4,432,128]{7,6,5,4,3,2,1,0:T(8,128)(2,1)}, bf16[2,2,2,4,2,4,432,128]{7,6,5,4,3,2,1,0:T(8,128)(2,1)S(1)}, u32[]{:S(2)}) %copy-start) | copy-done | bytes 28311576
  187.4 0.0 copy-start.1
  187.4 9.1 %copy-done.1 = bf16[2,2,2,4,2,4,432,128]{7,6,5,4,3,2,1,0:T(8,128)(2,1)S(1)} copy-done((bf16[2,2,2,4,2,4,432,128]{7,6,5,4,3,2,1,0:T(8,128)(2,1)S(1)}, bf16[2,2,2,4,2,4,432,128]{7,6,5,4,3,2,1,0:T(8,128)(2,1)}, u32[]{:S(2)}) %copy-start.1) | copy-done | bytes 28311576
  196.5 11.4 %write.1 = (bf16[2,4,4,2,576,128]{5,4,3,2,1,0:T(8,128)(2,1)}, bf16[2,4,4,2,576,128]{5,4,3,2,1,0:T(8,128)(2,1)}, bf16[2,4,4,2,576,128]{5,4,3,2,1,0:T(8,128)(2,1)}...) custom-call(bf16[2,2,2,4,2,4,432,128]{7,6,5,4,3,2,1,0:T(8,128)(2,1)S, ...), custom_call_target="tpu_custom_call" | custom-call | tf_op jit(solution)/shard_map/write/pallas_call | solution.py:463
Async XLA Ops:
  178.1 9.4 %copy-start = (bf16[2,2,2,4,2,4,432,128]{7,6,5,4,3,2,1,0:T(8,128)(2,1)}, bf16[2,2,2,4,2,4,432,128]{7,6,5,4,3,2,1,0:T(8,128)(2,1)S(1)}, u32[]{:S(2)}) copy-start(bf16[2,2,2,4,2,4,432,128]{7,6,5,4,3,2,1,0:T(8,128)(2,1)S(1)} %get-tuple-element.20.whole) | copy-start | bytes 84934656
  187.4 9.1 %copy-start.1 = (bf16[2,2,2,4,2,4,432,128]{7,6,5,4,3,2,1,0:T(8,128)(2,1)S(1)}, bf16[2,2,2,4,2,4,432,128]{7,6,5,4,3,2,1,0:T(8,128)(2,1)}, u32[]{:S(2)}) copy-start(bf16[2,2,2,4,2,4,432,128]{7,6,5,4,3,2,1,0:T(8,128)(2,1)} %copy-done) | copy-start | bytes 84934656

commit v2 on v1

v2 whole, which is shorter than its diff:
```python
import functools
import math

import jax
import jax.numpy as jnp
from jax import lax
from jax.experimental import pallas as pl
from jax.experimental.pallas import tpu as pltpu
from jax.sharding import PartitionSpec as P

LANES = 128
TILE = 8
CORES = 2
AXES = 2
HALVES = 2
QUARTERS = AXES * HALVES
F32, BF16 = jnp.float32, jnp.bfloat16


def tiled(a, *blocks):
    layers, rows, columns = a.shape
    a = a.reshape(layers, rows // TILE, TILE, columns // LANES, LANES).transpose(0, 1, 3, 2, 4)
    return a.reshape(layers, *blocks, rows * columns // (LANES * math.prod(blocks)), LANES)


def untiled(a, shape):
    layers, rows, columns = shape
    a = a.reshape(layers, rows // TILE, columns // LANES, TILE, LANES).transpose(0, 1, 3, 2, 4)
    return a.reshape(shape)


def steps(count, body):
    def run(i, carry):
        body(i)
        return carry

    lax.fori_loop(0, count, run, 0)


def exchange_kernel(n, side, *refs):
    g_refs, w_refs, m_refs, v_refs = (refs[i : i + 3] for i in (0, 3, 6, 9))
    whole, moments = refs[12:14]
    (land1, land2, grads, w_own, m_own, v_own, squares) = refs[14:21]
    load_sem, swap_first, swap_rest, arrivals, state_sem, sent = refs[21:]
    swap_sent, sent1, sent2, square_sent, square_came, out_sent1, out_sent2, pair_sent, pair_came = (sent.at[i] for i in range(9))
    kinds = len(g_refs)
    layers = g_refs[0].shape[0]
    rows = g_refs[0].shape[-2] // QUARTERS
    unit = kinds * rows

    me = lax.axis_index("dp")
    core = lax.rem(me, CORES)
    here = (lax.div(lax.div(me, CORES), side), lax.rem(lax.div(me, CORES), side))
    sibling = me + 1 - 2 * core

    def wrap(i):
        return lax.rem(i + 2 * side, side)

    def split(i):
        a, h = i // HALVES, i % HALVES
        return a, h, (1 - a) * here[0] + a * here[1], (1 - a) * here[1] + a * here[0]

    def chip(a, d, e):
        return (1 - a) * d + a * e, (1 - a) * e + a * d

    def device(a, d, e):
        x, y = chip(a, d, e)
        return (x * side + y) * CORES + core

    def remote(src, dst, send, recv, to):
        return pltpu.make_async_remote_copy(
            src_ref=src, dst_ref=dst, send_sem=send, recv_sem=recv, device_id={"dp": to}, device_id_type=pl.DeviceIdType.MESH
        )

    def quarter(i):
        return pl.ds(pl.multiple_of(i * rows, rows), rows)

    def away(s, h):
        return (2, 1 - 2 * h, 2 * h - 1, 0)[s]

    def wait(ref, sem):
        pltpu.make_async_copy(ref, ref, sem).wait()

    barrier = pltpu.get_barrier_semaphore()
    x, y = here
    beside_me = [sibling] + [device(0, wrap(x + i), wrap(y + j)) for i, j in ((1, 0), (-1, 0), (0, 1), (0, -1))]
    for to in beside_me:
        pl.semaphore_signal(barrier, inc=1, device_id={"dp": to}, device_id_type=pl.DeviceIdType.MESH)

    quarters = [(a, h) for a in range(AXES) for h in range(HALVES)]

    def blocks(of, kind, a, h, w):
        lines = pl.ds((a * HALVES + h) * rows, rows)
        d = wrap(here[a] + away(kind, h))
        src = g_refs[w].at[:, d, :, of, lines, :] if a == 0 else g_refs[w].at[:, :, d, of, lines, :]
        return src, (a, h, d, slice(None), slice(None), pl.ds(w * rows, rows), slice(None))

    for kind in range(4):
        for a, h in quarters:
            for w in range(kinds):
                src, at = blocks(core, kind, a, h, w)
                pltpu.make_async_copy(src, whole.at[(0, *at)], load_sem.at[kind]).start()

    def state_copies():
        mine = (slice(None), here[0], here[1], core)
        for w in range(kinds):
            yield pltpu.make_async_copy(w_refs[w].at[mine], w_own.at[w], state_sem.at[0])
            yield pltpu.make_async_copy(m_refs[w], m_own.at[w], state_sem.at[1])
            yield pltpu.make_async_copy(v_refs[w], v_own.at[w], state_sem.at[2])

    pl.semaphore_wait(barrier, len(beside_me))

    for s in range(4):

        def swap_one(i):
            a, h, p, q = split(i)
            d, e = wrap(p + 2), wrap(q + away(s, h))
            for w in range(kinds):
                src = g_refs[w].at[(slice(None), *chip(a, d, e), 1 - core, quarter(i), slice(None))]
                dst = whole.at[1, a, h, d, :, e, pl.ds(w * rows, rows), :]
                remote(src, dst, swap_sent, swap_first.at[i, s], sibling).start()

        steps(QUARTERS, swap_one)

    def swap_others():
        for kind in range(1, 4):
            for a, h in quarters:
                for w in range(kinds):
                    src, at = blocks(1 - core, kind, a, h, w)
                    remote(src, whole.at[(1, *at)], swap_sent, swap_rest.at[kind - 1], sibling).start()

    def wait_load(kind):
        wait(whole.at[0, :, :, 0], load_sem.at[kind])

    def wait_swap(kind):
        wait(whole.at[1, :, :, 0], swap_rest.at[kind - 1])

    def add(dst, *srcs):
        def piece(j):
            at = (j // kinds, quarter(j % kinds))
            total = srcs[0][at].astype(F32)
            for src in srcs[1:]:
                total += src[at].astype(F32)
            dst[at] = total.astype(BF16)

        steps(layers * kinds, piece)

    def toward(kind, p, h):
        return wrap(p + (2 * h - 1, 1 - 2 * h, 2 * h - 1)[kind])

    def arrival1(kind, a, h, s):
        return arrivals.at[a, h, (s, 8, 4 + s)[kind]]

    def pass1(kind, i, s):
        a, h, p, q = split(i)
        d, e = wrap(p + away(kind, h)), wrap(q + away(s, h))
        terms, others = whole.at[0, a, h, d, :, e], whole.at[1, a, h, d, :, e]
        to = device(a, toward(kind, p, h), q)
        return terms, others, remote(terms, land1.at[kind, a, h, s], sent1, arrival1(kind, a, h, s), to)

    wait_load(0)
    for s in range(4):

        def across_first(i):
            a, h, _, _ = split(i)
            wait(land2.at[0, 0, 0], swap_first.at[i, s])
            terms, others, copy = pass1(0, i, s)
            add(terms, terms, others)
            copy.start()

        steps(QUARTERS, across_first)
        if s == 0:
            swap_others()

    for kind in (1, 2):
        wait_load(kind)
        wait_swap(kind)
        for s in range(4):

            def start1(i):
                a, h, _, _ = split(i)
                terms, others, copy = pass1(kind, i, s)
                if kind == 2:
                    wait(land1.at[0, a, h, s], arrival1(0, a, h, s))
                    add(terms, terms, others, land1.at[0, a, h, s])
                else:
                    add(terms, terms, others)
                copy.start()

            steps(QUARTERS, start1)

    for copy in state_copies():
        copy.start()

    def arrival2(kind, a, h):
        return arrivals.at[a, h, 9 + kind]

    def pass2(kind, i):
        a, h, p, q = split(i)
        e = wrap(q + away(kind, h))
        return remote(whole.at[0, a, h, p, :, e], land2.at[kind, a, h], sent2, arrival2(kind, a, h), device(a, p, toward(kind, q, h)))

    wait_load(3)
    wait_swap(3)
    for kind in range(3):

        def start2(i):
            a, h, p, q = split(i)
            e = wrap(q + away(kind, h))
            if kind == 0:
                wait(land1.at[1, a, h], arrival1(1, a, h, 0))
            wait(land1.at[2, a, h, kind], arrival1(2, a, h, kind))
            terms = whole.at[0, a, h, p, :, e]
            srcs = [terms, whole.at[1, a, h, p, :, e], land1.at[1, a, h, kind], land1.at[2, a, h, kind]]
            if kind == 2:
                wait(land2.at[0, a, h], arrival2(0, a, h))
                srcs.append(land2.at[0, a, h])
            add(terms, *srcs)
            pass2(kind, i).start()

        steps(QUARTERS, start2)

    def finish(i, total):
        a, h, p, q = split(i)
        wait(land1.at[2, a, h, 3], arrival1(2, a, h, 3))
        for kind in (1, 2):
            wait(land2.at[kind, a, h], arrival2(kind, a, h))
        srcs = [whole.at[k, a, h, p, :, q] for k in range(2)] + [land1.at[k, a, h, 3] for k in (1, 2)] + [land2.at[k, a, h] for k in (1, 2)]

        def piece(j, total):
            at = (j // kinds, quarter(j % kinds))
            g = srcs[0][at].astype(F32)
            for src in srcs[1:]:
                g += src[at].astype(F32)
            g = g.astype(BF16)
            grads[a, h, j // kinds, quarter(j % kinds)] = g
            g = g.astype(F32)
            return total + jnp.sum((g * g).reshape(rows // TILE, TILE, LANES), axis=0)

        return lax.fori_loop(0, layers * kinds, piece, total)

    squares[me] = lax.fori_loop(0, QUARTERS, finish, jnp.zeros((TILE, LANES), F32))

    wait(land1, sent1)
    wait(land2, sent2)

    def square(i):
        remote(squares.at[me], squares.at[me], square_sent, square_came, lax.rem(me + 1 + i, n)).start()

    steps(n - 1, square)
    for i, ref in enumerate((w_own, m_own, v_own)):
        wait(ref, state_sem.at[i])
    wait(squares.at[pl.ds(0, n - 1)], square_came)
    total = lax.fori_loop(0, n, lambda i, t: t + squares[i], jnp.zeros((TILE, LANES), F32))
    total = jnp.sum(jnp.sum(total, axis=0, keepdims=True), axis=1, keepdims=True)
    count = n * layers * kinds * QUARTERS * rows * LANES
    factor = jnp.minimum(1.0, 0.5 * lax.rsqrt(total / count + 1e-30))

    def out2(i, d, e, k):
        a, h, p, q = split(i)
        ref = whole.at[0, a, h, d, :, e]
        remote(ref, ref, out_sent2, arrivals.at[a, h, d * side + e], device(a, wrap(p + k), q)).start()

    def out1(i, e, k):
        a, h, p, q = split(i)
        ref = whole.at[0, a, h, p, :, e]
        remote(ref, ref, out_sent1, arrivals.at[a, h, p * side + e], device(a, p, wrap(q + k))).start()

    def pair(i, d, e):
        a, h, _, _ = split(i)
        remote(whole.at[0, a, h, d, :, e], whole.at[1, a, h, d, :, e], pair_sent, pair_came, sibling).start()

    def arrived(i, d, e):
        a, h, _, _ = split(i)
        wait(whole.at[0, a, h, d, :, e], arrivals.at[a, h, d * side + e])

    def update(i):
        a, h, p, q = split(i)

        def piece(j):
            layer, w = j // kinds, j % kinds
            at = (w, layer, pl.ds(pl.multiple_of(i * rows, rows), rows))
            g = grads[a, h, layer, quarter(w)].astype(F32) * factor
            w_old = w_own[at].astype(F32)
            m = 0.9 * m_own[at] + 0.1 * g
            v = 0.95 * v_own[at] + 0.05 * g * g
            step = m * lax.rsqrt(v + 1e-8) + 0.1 * w_old
            moments[(0, *at)] = m
            moments[(1, *at)] = v
            whole[0, a, h, p, layer, q, quarter(w)] = (w_old - 0.02 * step).astype(BF16)

        steps(layers * kinds, piece)
        out1(i, q, 2 * h - 1)
        out2(i, p, q, 2 * h - 1)

    steps(QUARTERS, update)

    def own(i):
        _, h, p, q = split(i)
        out1(i, q, 1 - 2 * h)
        out2(i, p, q, 1 - 2 * h)
        pair(i, p, q)

    steps(QUARTERS, own)

    def place(r, h):
        return (0, 1 - 2 * h, 2 * h - 1, 2)[r]

    def column(r):
        def run(i):
            _, h, p, q = split(i)
            e = wrap(q + place(r, h))
            arrived(i, p, e)
            if r == 1:
                out1(i, e, 2 * h - 1)
            out2(i, p, e, 2 * h - 1)
            out2(i, p, e, 1 - 2 * h)
            pair(i, p, e)

        steps(QUARTERS, run)

    def beside(r):
        def run(i):
            _, h, p, q = split(i)
            e = wrap(q + place(r, h))
            d = wrap(p + 1 - 2 * h)
            arrived(i, d, e)
            out2(i, d, e, 2 * h - 1)
            pair(i, d, e)
            d = wrap(p + 2 * h - 1)
            arrived(i, d, e)
            pair(i, d, e)

        steps(QUARTERS, run)

    def across(r):
        def run(i):
            _, h, p, q = split(i)
            d, e = wrap(p + 2), wrap(q + place(r, h))
            arrived(i, d, e)
            pair(i, d, e)

        steps(QUARTERS, run)

    column(1)
    column(2)
    beside(0)
    column(3)
    beside(1)
    beside(2)
    across(0)
    beside(3)
    across(1)
    across(2)
    across(3)

    wait(whole.at[1], pair_came)
    wait(whole.at[0], pair_sent)
    wait(land1, out_sent2)
    wait(land2, out_sent1)
    wait(whole.at[1], swap_sent)
    wait(squares.at[pl.ds(0, n - 1)], square_sent)


def write_kernel(side, whole, moments, *refs):
    w_refs, m_refs, v_refs, sem = refs[:3], refs[3:6], refs[6:9], refs[9]
    kinds = len(w_refs)
    rows = w_refs[0].shape[-2] // QUARTERS
    core = lax.rem(lax.axis_index("dp"), CORES)

    def copies(d):
        for k in range(CORES):
            c = core if k == 0 else 1 - core
            for a in range(AXES):
                for h in range(HALVES):
                    lines = pl.ds((a * HALVES + h) * rows, rows)
                    for w in range(kinds):
                        dst = w_refs[w].at[:, d, :, c, lines, :] if a == 0 else w_refs[w].at[:, :, d, c, lines, :]
                        pltpu.make_async_copy(whole.at[k, a, h, d, :, :, pl.ds(w * rows, rows), :], dst, sem.at[0]).start()

    steps(side, copies)
    for w in range(kinds):
        pltpu.make_async_copy(moments.at[0, w], m_refs[w], sem.at[1]).start()
        pltpu.make_async_copy(moments.at[1, w], v_refs[w], sem.at[1]).start()
    pltpu.make_async_copy(whole, whole, sem.at[0]).wait()
    pltpu.make_async_copy(moments, moments, sem.at[1]).wait()


def solution(mesh):
    n = mesh.shape["dp"]
    side = math.isqrt(n // CORES)

    def step(*arrays):
        terms, weights, m, v = (arrays[i : i + 3] for i in (0, 3, 6, 9))
        kinds, layers = len(weights), weights[0].shape[0]
        g = [tiled(t[0], side, side, CORES) for t in terms]
        w = [tiled(a, side, side, CORES) for a in weights]
        states = [tiled(a) for a in (*m, *v)]
        block = g[0].shape[-2]
        rows = block // QUARTERS
        unit = kinds * rows
        hbm, vmem = pl.BlockSpec(memory_space=pltpu.HBM), pl.BlockSpec(memory_space=pltpu.VMEM)
        dma = pltpu.SemaphoreType.DMA
        piece = (AXES, HALVES)
        whole, moments = pl.pallas_call(
            functools.partial(exchange_kernel, n, side),
            out_shape=(
                pltpu.VMEM((CORES, *piece, side, layers, side, unit, LANES), BF16),
                pltpu.VMEM((2, kinds, layers, block, LANES), F32),
            ),
            in_specs=[hbm] * 12,
            out_specs=(vmem, vmem),
            scratch_shapes=[
                pltpu.VMEM((3, *piece, side, layers, unit, LANES), BF16),
                pltpu.VMEM((3, *piece, layers, unit, LANES), BF16),
                pltpu.VMEM((*piece, layers, unit, LANES), BF16),
                pltpu.VMEM((kinds, layers, block, LANES), BF16),
                pltpu.VMEM((kinds, layers, block, LANES), F32),
                pltpu.VMEM((kinds, layers, block, LANES), F32),
                pltpu.VMEM((n, TILE, LANES), F32),
                dma((4,)),
                dma((QUARTERS, 4)),
                dma((3,)),
                dma((*piece, side * side)),
                dma((3,)),
                dma((9,)),
            ],
            compiler_params=pltpu.CompilerParams(collective_id=0, has_side_effects=True, vmem_limit_bytes=33 << 20),
            name="exchange",
        )(*g, *w, *states)
        out = pl.pallas_call(
            functools.partial(write_kernel, side),
            out_shape=tuple(jax.ShapeDtypeStruct(a.shape, a.dtype) for a in (*w, *states)),
            in_specs=[vmem] * 2,
            out_specs=(hbm,) * 9,
            scratch_shapes=[dma((2,))],
            compiler_params=pltpu.CompilerParams(vmem_limit_bytes=1 << 20),
            name="write",
        )(*(pltpu.with_memory_space_constraint(a, pltpu.VMEM) for a in (whole, moments)))
        return tuple(untiled(o, a.shape) for o, a in zip(out, (*weights, *m, *v), strict=True))

    all_of, cut = P(None, None, None), P(None, "dp", None)
    return jax.shard_map(
        step,
        mesh=mesh,
        in_specs=(P(("rep", "dp"), None, None, None),) * 3 + (all_of,) * 3 + (cut,) * 6,
        out_specs=(P("rep", None, None),) * 3 + (P("rep", "dp", None),) * 6,
        check_vma=False,
    )
```

time: 208 us -> 178 us (0.86)
  local copies, waits for them, and re-layouts: 18.4 us -> 0 us
  Pallas kernels: 189 us -> 177 us
    unnamed x4 -> x0, local copies, waits for them, and re-layouts: 18.4 us -> none
    pallas_call x1, Pallas kernels: 177 us -> 167 us  [step(): pl.pallas_call(functools.partial(exchange_kernel, n, side), out_shape=(pl...]
where the time goes in v2:
time: 178 us
  Pallas kernels  177 us (99%)
    pallas_call x1, Pallas kernels, step(): pl.pallas_call(functools.partial(exchange_kernel, n, side), out_shape=(pl...  167 us
    pallas_call x1, Pallas kernels, step(): pl.pallas_call(functools.partial(write_kernel, side), out_shape=tuple((ja...  10.4 us

profile of v2, /device:TPU:97, one launch (start us, length us, event | category | flops | bytes accessed | tf_op | source)
XLA Modules:
  0.0 177.7 jit_solution(14342161958406822835)
XLA Ops:
  0.6 166.7 %exchange.1 = (bf16[2,2,2,4,2,4,432,128]{7,6,5,4,3,2,1,0:T(8,128)(2,1)S(1)}, f32[2,3,2,576,128]{4,3,2,1,0:T(8,128)S(1)}) custom-call(bf16[2,4,4,2,576,128]{5,4,3,2,1,0:T(8,128)(2,1)} %bitcast.105, bf16[2,4,4,2,576,128]{5,4,3,2,1,0:T(8,128)(2,1)} %bitcast.106, bf16[2,4,4,2,576,128]{5,4,3,2,1,0:T(8,128)(2,1)} %bitcast.107, ...), custom_call_target="tpu_custom_call" | custom-call | tf_op jit(solution)/shard_map/exchange/pallas_call | solution.py:405
  167.3 10.4 %write.1 = (bf16[2,4,4,2,576,128]{5,4,3,2,1,0:T(8,128)(2,1)}, bf16[2,4,4,2,576,128]{5,4,3,2,1,0:T(8,128)(2,1)}, bf16[2,4,4,2,576,128]{5,4,3,2,1,0:T(8,128)(2,1)}...) custom-call(bf16[2,2,2,4,2,4,432,128]{7,6,5,4,3,2,1,0:T(8,128)(2,1)S, ...), custom_call_target="tpu_custom_call" | custom-call | tf_op jit(solution)/shard_map/write/pallas_call | solution.py:431

commit v3 on v2

--- a/solution.py
+++ b/solution.py
@@ -1,4 +1,5 @@
 import functools
+import itertools
 import math
 
 import jax
@@ -40,8 +41,8 @@
 def exchange_kernel(n, side, *refs):
     g_refs, w_refs, m_refs, v_refs = (refs[i : i + 3] for i in (0, 3, 6, 9))
     whole, moments = refs[12:14]
-    (land1, land2, grads, w_own, m_own, v_own, squares) = refs[14:21]
-    load_sem, swap_first, swap_rest, arrivals, state_sem, sent = refs[21:]
+    land1, land2, partial, grads, w_own, m_own, v_own, squares = refs[14:22]
+    load_sem, swap_first, swap_rest, arrivals, last, state_sem, sent = refs[22:]
     swap_sent, sent1, sent2, square_sent, square_came, out_sent1, out_sent2, pair_sent, pair_came = (sent.at[i] for i in range(9))
     kinds = len(g_refs)
     layers = g_refs[0].shape[0]
@@ -95,7 +96,7 @@
         src = g_refs[w].at[:, d, :, of, lines, :] if a == 0 else g_refs[w].at[:, :, d, of, lines, :]
         return src, (a, h, d, slice(None), slice(None), pl.ds(w * rows, rows), slice(None))
 
-    for kind in range(4):
+    def load(kind):
         for a, h in quarters:
             for w in range(kinds):
                 src, at = blocks(core, kind, a, h, w)
@@ -108,11 +109,11 @@
             yield pltpu.make_async_copy(m_refs[w], m_own.at[w], state_sem.at[1])
             yield pltpu.make_async_copy(v_refs[w], v_own.at[w], state_sem.at[2])
 
+    load(0)
     pl.semaphore_wait(barrier, len(beside_me))
 
-    for s in range(4):
-
-        def swap_one(i):
+    def swap_across(s):
+        def one(i):
             a, h, p, q = split(i)
             d, e = wrap(p + 2), wrap(q + away(s, h))
             for w in range(kinds):
@@ -120,14 +121,16 @@
                 dst = whole.at[1, a, h, d, :, e, pl.ds(w * rows, rows), :]
                 remote(src, dst, swap_sent, swap_first.at[i, s], sibling).start()
 
-        steps(QUARTERS, swap_one)
-
-    def swap_others():
-        for kind in range(1, 4):
-            for a, h in quarters:
-                for w in range(kinds):
-                    src, at = blocks(1 - core, kind, a, h, w)
-                    remote(src, whole.at[(1, *at)], swap_sent, swap_rest.at[kind - 1], sibling).start()
+        steps(QUARTERS, one)
+
+    def swap(kind):
+        for a, h in quarters:
+            for w in range(kinds):
+                src, at = blocks(1 - core, kind, a, h, w)
+                remote(src, whole.at[(1, *at)], swap_sent, swap_rest.at[kind - 1], sibling).start()
+
+    swap_across(0)
+    swap_across(1)
 
     def wait_load(kind):
         wait(whole.at[0, :, :, 0], load_sem.at[kind])
@@ -170,7 +173,16 @@
 
         steps(QUARTERS, across_first)
         if s == 0:
-            swap_others()
+            swap_across(2)
+            swap_across(3)
+            load(1)
+        if s == 1:
+            swap(1)
+            load(2)
+        if s == 2:
+            swap(2)
+            load(3)
+            swap(3)
 
     for kind in (1, 2):
         wait_load(kind)
@@ -198,7 +210,10 @@
     def pass2(kind, i):
         a, h, p, q = split(i)
         e = wrap(q + away(kind, h))
-        return remote(whole.at[0, a, h, p, :, e], land2.at[kind, a, h], sent2, arrival2(kind, a, h), device(a, p, toward(kind, q, h)))
+        terms, to = whole.at[0, a, h, p, :, e], device(a, p, toward(kind, q, h))
+        if kind < 2:
+            return [remote(terms, land2.at[kind, a, h], sent2, arrival2(kind, a, h), to)]
+        return [remote(terms.at[k], land2.at[kind, a, h, k], sent2, arrival2(kind + k, a, h), to) for k in range(layers)]
 
     wait_load(3)
     wait_swap(3)
@@ -216,43 +231,59 @@
                 wait(land2.at[0, a, h], arrival2(0, a, h))
                 srcs.append(land2.at[0, a, h])
             add(terms, *srcs)
-            pass2(kind, i).start()
+            for copy in pass2(kind, i):
+                copy.start()
 
         steps(QUARTERS, start2)
 
-    def finish(i, total):
+    def all_but_last(i):
         a, h, p, q = split(i)
         wait(land1.at[2, a, h, 3], arrival1(2, a, h, 3))
-        for kind in (1, 2):
-            wait(land2.at[kind, a, h], arrival2(kind, a, h))
-        srcs = [whole.at[k, a, h, p, :, q] for k in range(2)] + [land1.at[k, a, h, 3] for k in (1, 2)] + [land2.at[k, a, h] for k in (1, 2)]
+        wait(land2.at[1, a, h], arrival2(1, a, h))
+        srcs = [whole.at[k, a, h, p, :, q] for k in range(2)] + [land1.at[k, a, h, 3] for k in (1, 2)] + [land2.at[1, a, h]]
+
+        def piece(j):
+            at = (j // kinds, quarter(j % kinds))
+            partial[(a, h, *at)] = sum(src[at].astype(F32) for src in srcs)
+
+        steps(layers * kinds, piece)
+
+    steps(QUARTERS, all_but_last)
+
+    def finish(i, total, layer):
+        a, h, _, _ = split(i)
+        wait(land2.at[2, a, h, layer], arrival2(2 + layer, a, h))
 
         def piece(j, total):
-            at = (j // kinds, quarter(j % kinds))
-            g = srcs[0][at].astype(F32)
-            for src in srcs[1:]:
-                g += src[at].astype(F32)
-            g = g.astype(BF16)
-            grads[a, h, j // kinds, quarter(j % kinds)] = g
+            at = (a, h, layer, quarter(j))
+            g = (partial[at] + land2[(2, *at)].astype(F32)).astype(BF16)
+            grads[at] = g
             g = g.astype(F32)
             return total + jnp.sum((g * g).reshape(rows // TILE, TILE, LANES), axis=0)
 
-        return lax.fori_loop(0, layers * kinds, piece, total)
-
-    squares[me] = lax.fori_loop(0, QUARTERS, finish, jnp.zeros((TILE, LANES), F32))
+        return lax.fori_loop(0, kinds, piece, total)
+
+    total = jnp.zeros((TILE, LANES), F32)
+    for layer in range(layers):
+        total = lax.fori_loop(0, QUARTERS, functools.partial(finish, layer=layer), total)
+    squares[me] = jnp.sum(total, axis=0, keepdims=True)
 
     wait(land1, sent1)
     wait(land2, sent2)
 
-    def square(i):
-        remote(squares.at[me], squares.at[me], square_sent, square_came, lax.rem(me + 1 + i, n)).start()
-
-    steps(n - 1, square)
+    def far(place):
+        return -min(place[0], side - place[0]) - min(place[1], side - place[1])
+
+    for dx, dy, dc in sorted(itertools.product(range(side), range(side), range(CORES)), key=far):
+        if not (dx or dy or dc):
+            continue
+        to = (wrap(x + dx) * side + wrap(y + dy)) * CORES + (core if dc == 0 else 1 - core)
+        remote(squares.at[me], squares.at[me], square_sent, square_came, to).start()
     for i, ref in enumerate((w_own, m_own, v_own)):
         wait(ref, state_sem.at[i])
     wait(squares.at[pl.ds(0, n - 1)], square_came)
-    total = lax.fori_loop(0, n, lambda i, t: t + squares[i], jnp.zeros((TILE, LANES), F32))
-    total = jnp.sum(jnp.sum(total, axis=0, keepdims=True), axis=1, keepdims=True)
+    total = lax.fori_loop(0, n, lambda i, t: t + squares[i], jnp.zeros((1, LANES), F32))
+    total = jnp.sum(total, axis=1, keepdims=True)
     count = n * layers * kinds * QUARTERS * rows * LANES
     factor = jnp.minimum(1.0, 0.5 * lax.rsqrt(total / count + 1e-30))
 
@@ -274,20 +305,21 @@
         a, h, _, _ = split(i)
         wait(whole.at[0, a, h, d, :, e], arrivals.at[a, h, d * side + e])
 
+    def stepped(i, j):
+        a, h, _, _ = split(i)
+        layer, w = j // kinds, j % kinds
+        at = (w, layer, pl.ds(pl.multiple_of(i * rows, rows), rows))
+        g = grads[a, h, layer, quarter(w)].astype(F32) * factor
+        return at, 0.9 * m_own[at] + 0.1 * g, 0.95 * v_own[at] + 0.05 * g * g
+
     def update(i):
         a, h, p, q = split(i)
 
         def piece(j):
-            layer, w = j // kinds, j % kinds
-            at = (w, layer, pl.ds(pl.multiple_of(i * rows, rows), rows))
-            g = grads[a, h, layer, quarter(w)].astype(F32) * factor
+            at, m, v = stepped(i, j)
             w_old = w_own[at].astype(F32)
-            m = 0.9 * m_own[at] + 0.1 * g
-            v = 0.95 * v_own[at] + 0.05 * g * g
             step = m * lax.rsqrt(v + 1e-8) + 0.1 * w_old
-            moments[(0, *at)] = m
-            moments[(1, *at)] = v
-            whole[0, a, h, p, layer, q, quarter(w)] = (w_old - 0.02 * step).astype(BF16)
+            whole[0, a, h, p, j // kinds, q, quarter(j % kinds)] = (w_old - 0.02 * step).astype(BF16)
 
         steps(layers * kinds, piece)
         out1(i, q, 2 * h - 1)
@@ -302,6 +334,16 @@
         pair(i, p, q)
 
     steps(QUARTERS, own)
+
+    def keep(i):
+        def piece(j):
+            at, m, v = stepped(i, j)
+            moments[(0, *at)] = m
+            moments[(1, *at)] = v
+
+        steps(layers * kinds, piece)
+
+    steps(QUARTERS, keep)
 
     def place(r, h):
         return (0, 1 - 2 * h, 2 * h - 1, 2)[r]
@@ -321,11 +363,16 @@
 
     def beside(r):
         def run(i):
-            _, h, p, q = split(i)
+            a, h, p, q = split(i)
             e = wrap(q + place(r, h))
             d = wrap(p + 1 - 2 * h)
             arrived(i, d, e)
-            out2(i, d, e, 2 * h - 1)
+            if r < 3:
+                out2(i, d, e, 2 * h - 1)
+            else:
+                for k in range(layers):
+                    ref = whole.at[0, a, h, d, k, e]
+                    remote(ref, ref, out_sent2, last.at[a, h, k], device(a, wrap(p + 2 * h - 1), q)).start()
             pair(i, d, e)
             d = wrap(p + 2 * h - 1)
             arrived(i, d, e)
@@ -339,6 +386,15 @@
             d, e = wrap(p + 2), wrap(q + place(r, h))
             arrived(i, d, e)
             pair(i, d, e)
+
+        steps(QUARTERS, run)
+
+    def across_last(k):
+        def run(i):
+            a, h, p, q = split(i)
+            d, e = wrap(p + 2), wrap(q + place(3, h))
+            wait(whole.at[0, a, h, d, k, e], last.at[a, h, k])
+            remote(whole.at[0, a, h, d, k, e], whole.at[1, a, h, d, k, e], pair_sent, pair_came, sibling).start()
 
         steps(QUARTERS, run)
 
@@ -352,7 +408,8 @@
     beside(3)
     across(1)
     across(2)
-    across(3)
+    for k in range(layers):
+        across_last(k)
 
     wait(whole.at[1], pair_came)
     wait(whole.at[0], pair_sent)
@@ -413,15 +470,17 @@
             scratch_shapes=[
                 pltpu.VMEM((3, *piece, side, layers, unit, LANES), BF16),
                 pltpu.VMEM((3, *piece, layers, unit, LANES), BF16),
+                pltpu.VMEM((*piece, layers, unit, LANES), F32),
                 pltpu.VMEM((*piece, layers, unit, LANES), BF16),
                 pltpu.VMEM((kinds, layers, block, LANES), BF16),
                 pltpu.VMEM((kinds, layers, block, LANES), F32),
                 pltpu.VMEM((kinds, layers, block, LANES), F32),
-                pltpu.VMEM((n, TILE, LANES), F32),
+                pltpu.VMEM((n, 1, LANES), F32),
                 dma((4,)),
                 dma((QUARTERS, 4)),
                 dma((3,)),
                 dma((*piece, side * side)),
+                dma((*piece, layers)),
                 dma((3,)),
                 dma((9,)),
             ],

time: 178 us -> 175 us (0.983)
  Pallas kernels: 177 us -> 175 us
    pallas_call x1, Pallas kernels: 167 us -> 164 us  [step(): pl.pallas_call(functools.partial(exchange_kernel, n, side), out_shape=(pl...]
where the time goes in v3:
time: 175 us
  Pallas kernels  175 us (100%)
    pallas_call x1, Pallas kernels, step(): pl.pallas_call(functools.partial(exchange_kernel, n, side), out_shape=(pl...  164 us
    pallas_call x1, Pallas kernels, step(): pl.pallas_call(functools.partial(write_kernel, side), out_shape=tuple((ja...  10.4 us

profile of v3, /device:TPU:97, one launch (start us, length us, event | category | flops | bytes accessed | tf_op | source)
XLA Modules:
  0.0 175.3 jit_solution(17531629234591220559)
XLA Ops:
  0.6 164.3 %exchange.1 = (bf16[2,2,2,4,2,4,432,128]{7,6,5,4,3,2,1,0:T(8,128)(2,1)S(1)}, f32[2,3,2,576,128]{4,3,2,1,0:T(8,128)S(1)}) custom-call(bf16[2,4,4,2,576,128]{5,4,3,2,1,0:T(8,128)(2,1)} %bitcast.105, bf16[2,4,4,2,576,128]{5,4,3,2,1,0:T(8,128)(2,1)} %bitcast.106, bf16[2,4,4,2,576,128]{5,4,3,2,1,0:T(8,128)(2,1)} %bitcast.107, ...), custom_call_target="tpu_custom_call" | custom-call | tf_op jit(solution)/shard_map/exchange/pallas_call | solution.py:462
  165.0 10.4 %write.1 = (bf16[2,4,4,2,576,128]{5,4,3,2,1,0:T(8,128)(2,1)}, bf16[2,4,4,2,576,128]{5,4,3,2,1,0:T(8,128)(2,1)}, bf16[2,4,4,2,576,128]{5,4,3,2,1,0:T(8,128)(2,1)}...) custom-call(bf16[2,2,2,4,2,4,432,128]{7,6,5,4,3,2,1,0:T(8,128)(2,1)S, ...), custom_call_target="tpu_custom_call" | custom-call | tf_op jit(solution)/shard_map/write/pallas_call | solution.py:490

commit v4 on v3

--- a/solution.py
+++ b/solution.py
@@ -42,7 +42,7 @@
     g_refs, w_refs, m_refs, v_refs = (refs[i : i + 3] for i in (0, 3, 6, 9))
     whole, moments = refs[12:14]
     land1, land2, partial, grads, w_own, m_own, v_own, squares = refs[14:22]
-    load_sem, swap_first, swap_rest, arrivals, last, state_sem, sent = refs[22:]
+    load_sem, swap_first, swap_next, swap_rest, arrivals, last, state_sem, sent = refs[22:]
     swap_sent, sent1, sent2, square_sent, square_came, out_sent1, out_sent2, pair_sent, pair_came = (sent.at[i] for i in range(9))
     kinds = len(g_refs)
     layers = g_refs[0].shape[0]
@@ -112,14 +112,16 @@
     load(0)
     pl.semaphore_wait(barrier, len(beside_me))
 
+    def swap_one(i, s, w, sem):
+        a, h, p, q = split(i)
+        d, e = wrap(p + 2), wrap(q + away(s, h))
+        src = g_refs[w].at[(slice(None), *chip(a, d, e), 1 - core, quarter(i), slice(None))]
+        remote(src, whole.at[1, a, h, d, :, e, pl.ds(w * rows, rows), :], swap_sent, sem, sibling).start()
+
     def swap_across(s):
         def one(i):
-            a, h, p, q = split(i)
-            d, e = wrap(p + 2), wrap(q + away(s, h))
             for w in range(kinds):
-                src = g_refs[w].at[(slice(None), *chip(a, d, e), 1 - core, quarter(i), slice(None))]
-                dst = whole.at[1, a, h, d, :, e, pl.ds(w * rows, rows), :]
-                remote(src, dst, swap_sent, swap_first.at[i, s], sibling).start()
+                swap_one(i, s, w, swap_next.at[s - 1])
 
         steps(QUARTERS, one)
 
@@ -129,7 +131,8 @@
                 src, at = blocks(1 - core, kind, a, h, w)
                 remote(src, whole.at[(1, *at)], swap_sent, swap_rest.at[kind - 1], sibling).start()
 
-    swap_across(0)
+    for w in range(kinds):
+        steps(QUARTERS, lambda i: swap_one(i, 0, w, swap_first.at[i, w]))
     swap_across(1)
 
     def wait_load(kind):
@@ -161,17 +164,33 @@
         to = device(a, toward(kind, p, h), q)
         return terms, others, remote(terms, land1.at[kind, a, h, s], sent1, arrival1(kind, a, h, s), to)
 
+    def across_piece(i, w):
+        a, h, p, q = split(i)
+        d, e = wrap(p + 2), wrap(q + away(0, h))
+        own, other = (whole.at[k, a, h, d, :, e, pl.ds(w * rows, rows)] for k in range(2))
+        wait(land2.at[0, 0, 0, :, pl.ds(0, rows)], swap_first.at[i, w])
+
+        def layer(j):
+            own[j] = (own[j].astype(F32) + other[j].astype(F32)).astype(BF16)
+
+        steps(layers, layer)
+        to = device(a, toward(0, p, h), q)
+        remote(own, land1.at[0, a, h, 0, :, pl.ds(w * rows, rows)], sent1, arrival1(0, a, h, 0), to).start()
+
     wait_load(0)
     for s in range(4):
-
-        def across_first(i):
-            a, h, _, _ = split(i)
-            wait(land2.at[0, 0, 0], swap_first.at[i, s])
-            terms, others, copy = pass1(0, i, s)
-            add(terms, terms, others)
-            copy.start()
-
-        steps(QUARTERS, across_first)
+        if s == 0:
+            for w in range(kinds):
+                steps(QUARTERS, lambda i: across_piece(i, w))
+        else:
+            wait(land2.at[0], swap_next.at[s - 1])
+
+            def across_first(i):
+                terms, others, copy = pass1(0, i, s)
+                add(terms, terms, others)
+                copy.start()
+
+            steps(QUARTERS, across_first)
         if s == 0:
             swap_across(2)
             swap_across(3)
@@ -213,7 +232,8 @@
         terms, to = whole.at[0, a, h, p, :, e], device(a, p, toward(kind, q, h))
         if kind < 2:
             return [remote(terms, land2.at[kind, a, h], sent2, arrival2(kind, a, h), to)]
-        return [remote(terms.at[k], land2.at[kind, a, h, k], sent2, arrival2(kind + k, a, h), to) for k in range(layers)]
+        pieces = [pl.ds(w * rows, rows) for w in range(kinds)]
+        return [remote(terms.at[:, at], land2.at[kind, a, h, :, at], sent2, last.at[a, h, w], to) for w, at in enumerate(pieces)]
 
     wait_load(3)
     wait_swap(3)
@@ -250,22 +270,22 @@
 
     steps(QUARTERS, all_but_last)
 
-    def finish(i, total, layer):
+    def finish(i, total, w):
         a, h, _, _ = split(i)
-        wait(land2.at[2, a, h, layer], arrival2(2 + layer, a, h))
+        wait(land2.at[2, a, h, :, pl.ds(w * rows, rows)], last.at[a, h, w])
 
         def piece(j, total):
-            at = (a, h, layer, quarter(j))
+            at = (a, h, j, pl.ds(w * rows, rows))
             g = (partial[at] + land2[(2, *at)].astype(F32)).astype(BF16)
             grads[at] = g
             g = g.astype(F32)
             return total + jnp.sum((g * g).reshape(rows // TILE, TILE, LANES), axis=0)
 
-        return lax.fori_loop(0, kinds, piece, total)
+        return lax.fori_loop(0, layers, piece, total)
 
     total = jnp.zeros((TILE, LANES), F32)
-    for layer in range(layers):
-        total = lax.fori_loop(0, QUARTERS, functools.partial(finish, layer=layer), total)
+    for w in range(kinds):
+        total = lax.fori_loop(0, QUARTERS, functools.partial(finish, w=w), total)
     squares[me] = jnp.sum(total, axis=0, keepdims=True)
 
     wait(land1, sent1)
@@ -287,23 +307,23 @@
     count = n * layers * kinds * QUARTERS * rows * LANES
     factor = jnp.minimum(1.0, 0.5 * lax.rsqrt(total / count + 1e-30))
 
-    def out2(i, d, e, k):
+    def out2(i, d, e, k, far=1):
         a, h, p, q = split(i)
         ref = whole.at[0, a, h, d, :, e]
-        remote(ref, ref, out_sent2, arrivals.at[a, h, d * side + e], device(a, wrap(p + k), q)).start()
+        remote(ref, ref, out_sent2, arrivals.at[a, h, far * side + e], device(a, wrap(p + k), q)).start()
 
     def out1(i, e, k):
         a, h, p, q = split(i)
         ref = whole.at[0, a, h, p, :, e]
-        remote(ref, ref, out_sent1, arrivals.at[a, h, p * side + e], device(a, p, wrap(q + k))).start()
+        remote(ref, ref, out_sent1, arrivals.at[a, h, e], device(a, p, wrap(q + k))).start()
 
     def pair(i, d, e):
         a, h, _, _ = split(i)
         remote(whole.at[0, a, h, d, :, e], whole.at[1, a, h, d, :, e], pair_sent, pair_came, sibling).start()
 
-    def arrived(i, d, e):
+    def arrived(i, e, far):
         a, h, _, _ = split(i)
-        wait(whole.at[0, a, h, d, :, e], arrivals.at[a, h, d * side + e])
+        wait(land2.at[0, 0] if far == 1 else land2.at[0, 0, 0], arrivals.at[a, h, far * side + e])
 
     def stepped(i, j):
         a, h, _, _ = split(i)
@@ -312,20 +332,23 @@
         g = grads[a, h, layer, quarter(w)].astype(F32) * factor
         return at, 0.9 * m_own[at] + 0.1 * g, 0.95 * v_own[at] + 0.05 * g * g
 
-    def update(i):
-        a, h, p, q = split(i)
-
-        def piece(j):
-            at, m, v = stepped(i, j)
+    def update(i, w):
+        a, h, p, q = split(i)
+
+        def layer(j):
+            at, m, v = stepped(i, j * kinds + w)
             w_old = w_own[at].astype(F32)
             step = m * lax.rsqrt(v + 1e-8) + 0.1 * w_old
-            whole[0, a, h, p, j // kinds, q, quarter(j % kinds)] = (w_old - 0.02 * step).astype(BF16)
-
-        steps(layers * kinds, piece)
-        out1(i, q, 2 * h - 1)
-        out2(i, p, q, 2 * h - 1)
-
-    steps(QUARTERS, update)
+            whole[0, a, h, p, j, q, pl.ds(w * rows, rows)] = (w_old - 0.02 * step).astype(BF16)
+
+        steps(layers, layer)
+        ref = whole.at[0, a, h, p, :, q, pl.ds(w * rows, rows)]
+        k = 2 * h - 1
+        remote(ref, ref, out_sent1, arrivals.at[a, h, q], device(a, p, wrap(q + k))).start()
+        remote(ref, ref, out_sent2, arrivals.at[a, h, side + q], device(a, wrap(p + k), q)).start()
+
+    for w in range(kinds):
+        steps(QUARTERS, lambda i: update(i, w))
 
     def own(i):
         _, h, p, q = split(i)
@@ -352,7 +375,7 @@
         def run(i):
             _, h, p, q = split(i)
             e = wrap(q + place(r, h))
-            arrived(i, p, e)
+            arrived(i, e, 0)
             if r == 1:
                 out1(i, e, 2 * h - 1)
             out2(i, p, e, 2 * h - 1)
@@ -366,37 +389,32 @@
             a, h, p, q = split(i)
             e = wrap(q + place(r, h))
             d = wrap(p + 1 - 2 * h)
-            arrived(i, d, e)
+            arrived(i, e, 1)
             if r < 3:
-                out2(i, d, e, 2 * h - 1)
+                out2(i, d, e, 2 * h - 1, 2)
             else:
-                for k in range(layers):
-                    ref = whole.at[0, a, h, d, k, e]
-                    remote(ref, ref, out_sent2, last.at[a, h, k], device(a, wrap(p + 2 * h - 1), q)).start()
+                for w in range(kinds):
+                    ref = whole.at[0, a, h, d, :, e, pl.ds(w * rows, rows)]
+                    remote(ref, ref, out_sent2, last.at[a, h, w], device(a, wrap(p + 2 * h - 1), q)).start()
             pair(i, d, e)
-            d = wrap(p + 2 * h - 1)
-            arrived(i, d, e)
-            pair(i, d, e)
+            pair(i, wrap(p + 2 * h - 1), e)
 
         steps(QUARTERS, run)
 
     def across(r):
         def run(i):
             _, h, p, q = split(i)
-            d, e = wrap(p + 2), wrap(q + place(r, h))
-            arrived(i, d, e)
-            pair(i, d, e)
+            e = wrap(q + place(r, h))
+            arrived(i, e, 2)
+            pair(i, wrap(p + 2), e)
 
         steps(QUARTERS, run)
 
-    def across_last(k):
-        def run(i):
-            a, h, p, q = split(i)
-            d, e = wrap(p + 2), wrap(q + place(3, h))
-            wait(whole.at[0, a, h, d, k, e], last.at[a, h, k])
-            remote(whole.at[0, a, h, d, k, e], whole.at[1, a, h, d, k, e], pair_sent, pair_came, sibling).start()
-
-        steps(QUARTERS, run)
+    def across_last(i, w):
+        a, h, p, q = split(i)
+        at = (a, h, wrap(p + 2), slice(None), wrap(q + place(3, h)), pl.ds(w * rows, rows))
+        wait(land2.at[0, 0, 0, :, pl.ds(0, rows)], last.at[a, h, w])
+        remote(whole.at[(0, *at)], whole.at[(1, *at)], pair_sent, pair_came, sibling).start()
 
     column(1)
     column(2)
@@ -408,8 +426,8 @@
     beside(3)
     across(1)
     across(2)
-    for k in range(layers):
-        across_last(k)
+    for w in range(kinds):
+        steps(QUARTERS, lambda i: across_last(i, w))
 
     wait(whole.at[1], pair_came)
     wait(whole.at[0], pair_sent)
@@ -477,10 +495,11 @@
                 pltpu.VMEM((kinds, layers, block, LANES), F32),
                 pltpu.VMEM((n, 1, LANES), F32),
                 dma((4,)),
-                dma((QUARTERS, 4)),
+                dma((QUARTERS, kinds)),
                 dma((3,)),
-                dma((*piece, side * side)),
-                dma((*piece, layers)),
+                dma((3,)),
+                dma((*piece, 3 * side)),
+                dma((*piece, kinds)),
                 dma((3,)),
                 dma((9,)),
             ],

time: 175 us -> 174 us (level)
  Pallas kernels: 175 us -> 173 us
where the time goes in v4:
time: 174 us
  Pallas kernels  173 us (99%)
    pallas_call x1, Pallas kernels, step(): pl.pallas_call(functools.partial(exchange_kernel, n, side), out_shape=(pl...  163 us
    pallas_call x1, Pallas kernels, step(): pl.pallas_call(functools.partial(write_kernel, side), out_shape=tuple((ja...  10.4 us

profile of v4, /device:TPU:97, one launch (start us, length us, event | category | flops | bytes accessed | tf_op | source)
XLA Modules:
  0.0 173.9 jit_solution(11639005583994437616)
XLA Ops:
  0.6 162.9 %exchange.1 = (bf16[2,2,2,4,2,4,432,128]{7,6,5,4,3,2,1,0:T(8,128)(2,1)S(1)}, f32[2,3,2,576,128]{4,3,2,1,0:T(8,128)S(1)}) custom-call(bf16[2,4,4,2,576,128]{5,4,3,2,1,0:T(8,128)(2,1)} %bitcast.105, bf16[2,4,4,2,576,128]{5,4,3,2,1,0:T(8,128)(2,1)} %bitcast.106, bf16[2,4,4,2,576,128]{5,4,3,2,1,0:T(8,128)(2,1)} %bitcast.107, ...), custom_call_target="tpu_custom_call" | custom-call | tf_op jit(solution)/shard_map/exchange/pallas_call | solution.py:480
  163.5 10.4 %write.1 = (bf16[2,4,4,2,576,128]{5,4,3,2,1,0:T(8,128)(2,1)}, bf16[2,4,4,2,576,128]{5,4,3,2,1,0:T(8,128)(2,1)}, bf16[2,4,4,2,576,128]{5,4,3,2,1,0:T(8,128)(2,1)}...) custom-call(bf16[2,2,2,4,2,4,432,128]{7,6,5,4,3,2,1,0:T(8,128)(2,1)S, ...), custom_call_target="tpu_custom_call" | custom-call | tf_op jit(solution)/shard_map/write/pallas_call | solution.py:509

commit v5 on v4

--- a/solution.py
+++ b/solution.py
@@ -11,6 +11,7 @@
 
 LANES = 128
 TILE = 8
+KINDS = 3
 CORES = 2
 AXES = 2
 HALVES = 2
@@ -39,10 +40,26 @@
 
 
 def exchange_kernel(n, side, *refs):
+    kinds, dma, piece = KINDS, pltpu.SemaphoreType.DMA, (AXES, HALVES)
+    pl.run_scoped(
+        lambda *sems: exchange(n, side, *refs, *sems),
+        dma((4,)),
+        dma((3,)),
+        dma((QUARTERS, kinds)),
+        dma((3,)),
+        dma((3,)),
+        dma((*piece, 3 * side)),
+        dma((*piece, kinds)),
+        dma((3,)),
+        dma((9,)),
+    )
+
+
+def exchange(n, side, *refs):
     g_refs, w_refs, m_refs, v_refs = (refs[i : i + 3] for i in (0, 3, 6, 9))
     whole, moments = refs[12:14]
     land1, land2, partial, grads, w_own, m_own, v_own, squares = refs[14:22]
-    load_sem, swap_first, swap_next, swap_rest, arrivals, last, state_sem, sent = refs[22:]
+    load_first, load_sem, swap_first, swap_next, swap_rest, arrivals, last, state_sem, sent = refs[22:]
     swap_sent, sent1, sent2, square_sent, square_came, out_sent1, out_sent2, pair_sent, pair_came = (sent.at[i] for i in range(9))
     kinds = len(g_refs)
     layers = g_refs[0].shape[0]
@@ -100,7 +117,7 @@
         for a, h in quarters:
             for w in range(kinds):
                 src, at = blocks(core, kind, a, h, w)
-                pltpu.make_async_copy(src, whole.at[(0, *at)], load_sem.at[kind]).start()
+                pltpu.make_async_copy(src, whole.at[(0, *at)], load_sem.at[kind - 1]).start()
 
     def state_copies():
         mine = (slice(None), here[0], here[1], core)
@@ -109,14 +126,25 @@
             yield pltpu.make_async_copy(m_refs[w], m_own.at[w], state_sem.at[1])
             yield pltpu.make_async_copy(v_refs[w], v_own.at[w], state_sem.at[2])
 
-    load(0)
+    def across_at(i, s, w, of):
+        a, h, p, q = split(i)
+        d, e = wrap(p + 2), wrap(q + away(s, h))
+        return g_refs[w].at[(slice(None), *chip(a, d, e), of, quarter(i), slice(None))], (a, h, d, slice(None), e, pl.ds(w * rows, rows))
+
+    def load_across(s):
+        def one(i):
+            for w in range(kinds):
+                src, at = across_at(i, s, w, core)
+                pltpu.make_async_copy(src, whole.at[(0, *at)], load_first.at[s]).start()
+
+        steps(QUARTERS, one)
+
+    load_across(0)
     pl.semaphore_wait(barrier, len(beside_me))
 
     def swap_one(i, s, w, sem):
-        a, h, p, q = split(i)
-        d, e = wrap(p + 2), wrap(q + away(s, h))
-        src = g_refs[w].at[(slice(None), *chip(a, d, e), 1 - core, quarter(i), slice(None))]
-        remote(src, whole.at[1, a, h, d, :, e, pl.ds(w * rows, rows), :], swap_sent, sem, sibling).start()
+        src, at = across_at(i, s, w, 1 - core)
+        remote(src, whole.at[(1, *at)], swap_sent, sem, sibling).start()
 
     def swap_across(s):
         def one(i):
@@ -133,10 +161,11 @@
 
     for w in range(kinds):
         steps(QUARTERS, lambda i: swap_one(i, 0, w, swap_first.at[i, w]))
+    load_across(1)
     swap_across(1)
 
     def wait_load(kind):
-        wait(whole.at[0, :, :, 0], load_sem.at[kind])
+        wait(whole.at[0, :, :, 0], load_sem.at[kind - 1])
 
     def wait_swap(kind):
         wait(whole.at[1, :, :, 0], swap_rest.at[kind - 1])
@@ -177,8 +206,8 @@
         to = device(a, toward(0, p, h), q)
         remote(own, land1.at[0, a, h, 0, :, pl.ds(w * rows, rows)], sent1, arrival1(0, a, h, 0), to).start()
 
-    wait_load(0)
     for s in range(4):
+        wait(land2.at[0], load_first.at[s])
         if s == 0:
             for w in range(kinds):
                 steps(QUARTERS, lambda i: across_piece(i, w))
@@ -192,7 +221,9 @@
 
             steps(QUARTERS, across_first)
         if s == 0:
+            load_across(2)
             swap_across(2)
+            load_across(3)
             swap_across(3)
             load(1)
         if s == 1:
@@ -302,8 +333,7 @@
     for i, ref in enumerate((w_own, m_own, v_own)):
         wait(ref, state_sem.at[i])
     wait(squares.at[pl.ds(0, n - 1)], square_came)
-    total = lax.fori_loop(0, n, lambda i, t: t + squares[i], jnp.zeros((1, LANES), F32))
-    total = jnp.sum(total, axis=1, keepdims=True)
+    total = jnp.sum(jnp.sum(squares[...], axis=0), axis=1, keepdims=True)
     count = n * layers * kinds * QUARTERS * rows * LANES
     factor = jnp.minimum(1.0, 0.5 * lax.rsqrt(total / count + 1e-30))
 
@@ -494,14 +524,6 @@
                 pltpu.VMEM((kinds, layers, block, LANES), F32),
                 pltpu.VMEM((kinds, layers, block, LANES), F32),
                 pltpu.VMEM((n, 1, LANES), F32),
-                dma((4,)),
-                dma((QUARTERS, kinds)),
-                dma((3,)),
-                dma((3,)),
-                dma((*piece, 3 * side)),
-                dma((*piece, kinds)),
-                dma((3,)),
-                dma((9,)),
             ],
             compiler_params=pltpu.CompilerParams(collective_id=0, has_side_effects=True, vmem_limit_bytes=33 << 20),
             name="exchange",

time: 174 us -> 173 us (level)
  no operation moved by 1% of the time
where the time goes in v5:
time: 173 us
  Pallas kernels  172 us (99%)
    pallas_call x1, Pallas kernels, step(): pl.pallas_call(functools.partial(exchange_kernel, n, side), out_shape=(pl...  162 us
    pallas_call x1, Pallas kernels, step(): pl.pallas_call(functools.partial(write_kernel, side), out_shape=tuple((ja...  10.3 us

profile of v5, /device:TPU:97, one launch (start us, length us, event | category | flops | bytes accessed | tf_op | source)
XLA Modules:
  0.0 172.7 jit_solution(9340856715053807595)
XLA Ops:
  0.6 161.8 %exchange.1 = (bf16[2,2,2,4,2,4,432,128]{7,6,5,4,3,2,1,0:T(8,128)(2,1)S(1)}, f32[2,3,2,576,128]{4,3,2,1,0:T(8,128)S(1)}) custom-call(bf16[2,4,4,2,576,128]{5,4,3,2,1,0:T(8,128)(2,1)} %bitcast.105, bf16[2,4,4,2,576,128]{5,4,3,2,1,0:T(8,128)(2,1)} %bitcast.106, bf16[2,4,4,2,576,128]{5,4,3,2,1,0:T(8,128)(2,1)} %bitcast.107, ...), custom_call_target="tpu_custom_call" | custom-call | tf_op jit(solution)/shard_map/exchange/pallas_call | solution.py:510
  162.4 10.3 %write.1 = (bf16[2,4,4,2,576,128]{5,4,3,2,1,0:T(8,128)(2,1)}, bf16[2,4,4,2,576,128]{5,4,3,2,1,0:T(8,128)(2,1)}, bf16[2,4,4,2,576,128]{5,4,3,2,1,0:T(8,128)(2,1)}...) custom-call(bf16[2,2,2,4,2,4,432,128]{7,6,5,4,3,2,1,0:T(8,128)(2,1)S, ...), custom_call_target="tpu_custom_call" | custom-call | tf_op jit(solution)/shard_map/write/pallas_call | solution.py:531

commit v6 on v5

--- a/solution.py
+++ b/solution.py
@@ -40,16 +40,16 @@
 
 
 def exchange_kernel(n, side, *refs):
-    kinds, dma, piece = KINDS, pltpu.SemaphoreType.DMA, (AXES, HALVES)
+    kinds, layers, dma, piece = KINDS, refs[0].shape[0], pltpu.SemaphoreType.DMA, (AXES, HALVES)
     pl.run_scoped(
         lambda *sems: exchange(n, side, *refs, *sems),
         dma((4,)),
         dma((3,)),
-        dma((QUARTERS, kinds)),
+        dma((QUARTERS, layers, kinds)),
         dma((3,)),
         dma((3,)),
         dma((*piece, 3 * side)),
-        dma((*piece, kinds)),
+        dma((*piece, layers, kinds)),
         dma((3,)),
         dma((9,)),
     )
@@ -126,10 +126,12 @@
             yield pltpu.make_async_copy(m_refs[w], m_own.at[w], state_sem.at[1])
             yield pltpu.make_async_copy(v_refs[w], v_own.at[w], state_sem.at[2])
 
-    def across_at(i, s, w, of):
+    pieces = list(itertools.product(range(layers), range(kinds)))
+
+    def across_at(i, s, w, of, layer=slice(None)):
         a, h, p, q = split(i)
         d, e = wrap(p + 2), wrap(q + away(s, h))
-        return g_refs[w].at[(slice(None), *chip(a, d, e), of, quarter(i), slice(None))], (a, h, d, slice(None), e, pl.ds(w * rows, rows))
+        return g_refs[w].at[(layer, *chip(a, d, e), of, quarter(i), slice(None))], (a, h, d, layer, e, pl.ds(w * rows, rows))
 
     def load_across(s):
         def one(i):
@@ -142,8 +144,8 @@
     load_across(0)
     pl.semaphore_wait(barrier, len(beside_me))
 
-    def swap_one(i, s, w, sem):
-        src, at = across_at(i, s, w, 1 - core)
+    def swap_one(i, s, w, sem, layer=slice(None)):
+        src, at = across_at(i, s, w, 1 - core, layer)
         remote(src, whole.at[(1, *at)], swap_sent, sem, sibling).start()
 
     def swap_across(s):
@@ -159,8 +161,8 @@
                 src, at = blocks(1 - core, kind, a, h, w)
                 remote(src, whole.at[(1, *at)], swap_sent, swap_rest.at[kind - 1], sibling).start()
 
-    for w in range(kinds):
-        steps(QUARTERS, lambda i: swap_one(i, 0, w, swap_first.at[i, w]))
+    for layer, w in pieces:
+        steps(QUARTERS, lambda i: swap_one(i, 0, w, swap_first.at[i, layer, w], layer))
     load_across(1)
     swap_across(1)
 
@@ -193,24 +195,22 @@
         to = device(a, toward(kind, p, h), q)
         return terms, others, remote(terms, land1.at[kind, a, h, s], sent1, arrival1(kind, a, h, s), to)
 
-    def across_piece(i, w):
+    a_piece = land2.at[0, 0, 0, 0, pl.ds(0, rows)]
+
+    def across_piece(i, layer, w):
         a, h, p, q = split(i)
         d, e = wrap(p + 2), wrap(q + away(0, h))
-        own, other = (whole.at[k, a, h, d, :, e, pl.ds(w * rows, rows)] for k in range(2))
-        wait(land2.at[0, 0, 0, :, pl.ds(0, rows)], swap_first.at[i, w])
-
-        def layer(j):
-            own[j] = (own[j].astype(F32) + other[j].astype(F32)).astype(BF16)
-
-        steps(layers, layer)
+        own, other = (whole.at[k, a, h, d, layer, e, pl.ds(w * rows, rows)] for k in range(2))
+        wait(a_piece, swap_first.at[i, layer, w])
+        own[...] = (own[...].astype(F32) + other[...].astype(F32)).astype(BF16)
         to = device(a, toward(0, p, h), q)
-        remote(own, land1.at[0, a, h, 0, :, pl.ds(w * rows, rows)], sent1, arrival1(0, a, h, 0), to).start()
+        remote(own, land1.at[0, a, h, 0, layer, pl.ds(w * rows, rows)], sent1, arrival1(0, a, h, 0), to).start()
 
     for s in range(4):
         wait(land2.at[0], load_first.at[s])
         if s == 0:
-            for w in range(kinds):
-                steps(QUARTERS, lambda i: across_piece(i, w))
+            for layer, w in pieces:
+                steps(QUARTERS, lambda i: across_piece(i, layer, w))
         else:
             wait(land2.at[0], swap_next.at[s - 1])
 
@@ -263,8 +263,8 @@
         terms, to = whole.at[0, a, h, p, :, e], device(a, p, toward(kind, q, h))
         if kind < 2:
             return [remote(terms, land2.at[kind, a, h], sent2, arrival2(kind, a, h), to)]
-        pieces = [pl.ds(w * rows, rows) for w in range(kinds)]
-        return [remote(terms.at[:, at], land2.at[kind, a, h, :, at], sent2, last.at[a, h, w], to) for w, at in enumerate(pieces)]
+        parts = [(layer, pl.ds(w * rows, rows), last.at[a, h, layer, w]) for layer, w in pieces]
+        return [remote(terms.at[layer, at], land2.at[kind, a, h, layer, at], sent2, sem, to) for layer, at, sem in parts]
 
     wait_load(3)
     wait_swap(3)
@@ -301,22 +301,18 @@
 
     steps(QUARTERS, all_but_last)
 
-    def finish(i, total, w):
+    def finish(i, total, layer, w):
         a, h, _, _ = split(i)
-        wait(land2.at[2, a, h, :, pl.ds(w * rows, rows)], last.at[a, h, w])
-
-        def piece(j, total):
-            at = (a, h, j, pl.ds(w * rows, rows))
-            g = (partial[at] + land2[(2, *at)].astype(F32)).astype(BF16)
-            grads[at] = g
-            g = g.astype(F32)
-            return total + jnp.sum((g * g).reshape(rows // TILE, TILE, LANES), axis=0)
-
-        return lax.fori_loop(0, layers, piece, total)
+        wait(a_piece, last.at[a, h, layer, w])
+        at = (a, h, layer, pl.ds(w * rows, rows))
+        g = (partial[at] + land2[(2, *at)].astype(F32)).astype(BF16)
+        grads[at] = g
+        g = g.astype(F32)
+        return total + jnp.sum((g * g).reshape(rows // TILE, TILE, LANES), axis=0)
 
     total = jnp.zeros((TILE, LANES), F32)
-    for w in range(kinds):
-        total = lax.fori_loop(0, QUARTERS, functools.partial(finish, w=w), total)
+    for layer, w in pieces:
+        total = lax.fori_loop(0, QUARTERS, functools.partial(finish, layer=layer, w=w), total)
     squares[me] = jnp.sum(total, axis=0, keepdims=True)
 
     wait(land1, sent1)
@@ -362,23 +358,19 @@
         g = grads[a, h, layer, quarter(w)].astype(F32) * factor
         return at, 0.9 * m_own[at] + 0.1 * g, 0.95 * v_own[at] + 0.05 * g * g
 
-    def update(i, w):
-        a, h, p, q = split(i)
-
-        def layer(j):
-            at, m, v = stepped(i, j * kinds + w)
-            w_old = w_own[at].astype(F32)
-            step = m * lax.rsqrt(v + 1e-8) + 0.1 * w_old
-            whole[0, a, h, p, j, q, pl.ds(w * rows, rows)] = (w_old - 0.02 * step).astype(BF16)
-
-        steps(layers, layer)
-        ref = whole.at[0, a, h, p, :, q, pl.ds(w * rows, rows)]
+    def update(i, layer, w):
+        a, h, p, q = split(i)
+        at, m, v = stepped(i, layer * kinds + w)
+        w_old = w_own[at].astype(F32)
+        step = m * lax.rsqrt(v + 1e-8) + 0.1 * w_old
+        ref = whole.at[0, a, h, p, layer, q, pl.ds(w * rows, rows)]
+        ref[...] = (w_old - 0.02 * step).astype(BF16)
         k = 2 * h - 1
         remote(ref, ref, out_sent1, arrivals.at[a, h, q], device(a, p, wrap(q + k))).start()
         remote(ref, ref, out_sent2, arrivals.at[a, h, side + q], device(a, wrap(p + k), q)).start()
 
-    for w in range(kinds):
-        steps(QUARTERS, lambda i: update(i, w))
+    for layer, w in pieces:
+        steps(QUARTERS, lambda i: update(i, layer, w))
 
     def own(i):
         _, h, p, q = split(i)
@@ -423,9 +415,9 @@
             if r < 3:
                 out2(i, d, e, 2 * h - 1, 2)
             else:
-                for w in range(kinds):
-                    ref = whole.at[0, a, h, d, :, e, pl.ds(w * rows, rows)]
-                    remote(ref, ref, out_sent2, last.at[a, h, w], device(a, wrap(p + 2 * h - 1), q)).start()
+                for layer, w in pieces:
+                    ref = whole.at[0, a, h, d, layer, e, pl.ds(w * rows, rows)]
+                    remote(ref, ref, out_sent2, last.at[a, h, layer, w], device(a, wrap(p + 2 * h - 1), q)).start()
             pair(i, d, e)
             pair(i, wrap(p + 2 * h - 1), e)
 
@@ -440,10 +432,10 @@
 
         steps(QUARTERS, run)
 
-    def across_last(i, w):
-        a, h, p, q = split(i)
-        at = (a, h, wrap(p + 2), slice(None), wrap(q + place(3, h)), pl.ds(w * rows, rows))
-        wait(land2.at[0, 0, 0, :, pl.ds(0, rows)], last.at[a, h, w])
+    def across_last(i, layer, w):
+        a, h, p, q = split(i)
+        at = (a, h, wrap(p + 2), layer, wrap(q + place(3, h)), pl.ds(w * rows, rows))
+        wait(a_piece, last.at[a, h, layer, w])
         remote(whole.at[(0, *at)], whole.at[(1, *at)], pair_sent, pair_came, sibling).start()
 
     column(1)
@@ -456,8 +448,8 @@
     beside(3)
     across(1)
     across(2)
-    for w in range(kinds):
-        steps(QUARTERS, lambda i: across_last(i, w))
+    for layer, w in pieces:
+        steps(QUARTERS, lambda i: across_last(i, layer, w))
 
     wait(whole.at[1], pair_came)
     wait(whole.at[0], pair_sent)

time: 173 us -> 173 us (level)
  no operation moved by 1% of the time
where the time goes in v6:
time: 173 us; the launch traced here: 172 us
  Pallas kernels  172 us (99%)
    pallas_call x1, Pallas kernels, step(): pl.pallas_call(functools.partial(exchange_kernel, n, side), out_shape=(pl...  162 us
    pallas_call x1, Pallas kernels, step(): pl.pallas_call(functools.partial(write_kernel, side), out_shape=tuple((ja...  10.3 us

profile of v6, /device:TPU:97, one launch (start us, length us, event | category | flops | bytes accessed | tf_op | source)
XLA Modules:
  0.0 172.5 jit_solution(13425025469018016367)
XLA Ops:
  0.6 161.5 %exchange.1 = (bf16[2,2,2,4,2,4,432,128]{7,6,5,4,3,2,1,0:T(8,128)(2,1)S(1)}, f32[2,3,2,576,128]{4,3,2,1,0:T(8,128)S(1)}) custom-call(bf16[2,4,4,2,576,128]{5,4,3,2,1,0:T(8,128)(2,1)} %bitcast.105, bf16[2,4,4,2,576,128]{5,4,3,2,1,0:T(8,128)(2,1)} %bitcast.106, bf16[2,4,4,2,576,128]{5,4,3,2,1,0:T(8,128)(2,1)} %bitcast.107, ...), custom_call_target="tpu_custom_call" | custom-call | tf_op jit(solution)/shard_map/exchange/pallas_call | solution.py:502
  162.2 10.3 %write.1 = (bf16[2,4,4,2,576,128]{5,4,3,2,1,0:T(8,128)(2,1)}, bf16[2,4,4,2,576,128]{5,4,3,2,1,0:T(8,128)(2,1)}, bf16[2,4,4,2,576,128]{5,4,3,2,1,0:T(8,128)(2,1)}...) custom-call(bf16[2,2,2,4,2,4,432,128]{7,6,5,4,3,2,1,0:T(8,128)(2,1)S, ...), custom_call_target="tpu_custom_call" | custom-call | tf_op jit(solution)/shard_map/write/pallas_call | solution.py:523

commit v7 on v6

--- a/solution.py
+++ b/solution.py
@@ -163,8 +163,6 @@
 
     for layer, w in pieces:
         steps(QUARTERS, lambda i: swap_one(i, 0, w, swap_first.at[i, layer, w], layer))
-    load_across(1)
-    swap_across(1)
 
     def wait_load(kind):
         wait(whole.at[0, :, :, 0], load_sem.at[kind - 1])
@@ -221,6 +219,8 @@
 
             steps(QUARTERS, across_first)
         if s == 0:
+            load_across(1)
+            swap_across(1)
             load_across(2)
             swap_across(2)
             load_across(3)

time: 173 us -> 172 us (level)
  no operation moved by 1% of the time
where the time goes in v7:
time: 172 us
  Pallas kernels  172 us (100%)
    pallas_call x1, Pallas kernels, step(): pl.pallas_call(functools.partial(exchange_kernel, n, side), out_shape=(pl...  161 us
    pallas_call x1, Pallas kernels, step(): pl.pallas_call(functools.partial(write_kernel, side), out_shape=tuple((ja...  10.3 us

profile of v7, /device:TPU:97, one launch (start us, length us, event | category | flops | bytes accessed | tf_op | source)
XLA Modules:
  0.0 172.2 jit_solution(4549271812460599694)
XLA Ops:
  0.6 161.2 %exchange.1 = (bf16[2,2,2,4,2,4,432,128]{7,6,5,4,3,2,1,0:T(8,128)(2,1)S(1)}, f32[2,3,2,576,128]{4,3,2,1,0:T(8,128)S(1)}) custom-call(bf16[2,4,4,2,576,128]{5,4,3,2,1,0:T(8,128)(2,1)} %bitcast.105, bf16[2,4,4,2,576,128]{5,4,3,2,1,0:T(8,128)(2,1)} %bitcast.106, bf16[2,4,4,2,576,128]{5,4,3,2,1,0:T(8,128)(2,1)} %bitcast.107, ...), custom_call_target="tpu_custom_call" | custom-call | tf_op jit(solution)/shard_map/exchange/pallas_call | solution.py:502
  161.9 10.3 %write.1 = (bf16[2,4,4,2,576,128]{5,4,3,2,1,0:T(8,128)(2,1)}, bf16[2,4,4,2,576,128]{5,4,3,2,1,0:T(8,128)(2,1)}, bf16[2,4,4,2,576,128]{5,4,3,2,1,0:T(8,128)(2,1)}...) custom-call(bf16[2,2,2,4,2,4,432,128]{7,6,5,4,3,2,1,0:T(8,128)(2,1)S, ...), custom_call_target="tpu_custom_call" | custom-call | tf_op jit(solution)/shard_map/write/pallas_call | solution.py:523
